TPU v7x, 32 devices: a whole 2x2x4 slice. The times are simulated.
32 devices in a mesh: section: 4 (over y, core), mp: 8 (over z, x).
Axes of the slice: x: 2, y: 2, z: 4, core: 2. Of those that a mesh axis runs over, the one named last changes fastest.
Arguments:
- arriving: bfloat16 [4, 768, 8192], P('section', None, 'mp'), may hold values from -6 to 6
- norm_gain: bfloat16 [4, 8192], P('section'), may hold values from 0.099609375 to 1.8984375
- w_query: bfloat16 [4, 2048, 8192], P('section', 'mp'), may hold values from -26 to 26
- w_key: bfloat16 [4, 1024, 8192], P('section', 'mp'), may hold values from -1 to 1
- w_value: bfloat16 [4, 1024, 8192], P('section', 'mp'), may hold values from -0.25 to 0.25
- w_out: bfloat16 [4, 2048, 8192], P('section', 'mp'), may hold values from -0.125 to 0.125
Outputs:
- attended: bfloat16 [4, 768, 8192], P('section', 'mp')
- stream_next: bfloat16 [4, 768, 8192], P('section', 'mp')
All inputs are finite; a program needn't handle non-finite values.
Results may differ from a plain program's by a relative error of at most 0.017.
Values may be sent and summed in bfloat16 or wider, within the bound.
A program may use at most 128 MiB of HBM per device.

v0:
```python
import functools
import math

import jax
import jax.numpy as jnp
import numpy as np
from jax import lax
from jax.experimental import pallas as pl
from jax.experimental.pallas import tpu as pltpu
from jax.sharding import PartitionSpec as P

HD = 128
KV_HEADS = 8
ROPE_BASE = 500000.0
NORM_EPS = 1e-05
MESH = pl.DeviceIdType.MESH
VMEM_LIMIT = 63500000


def ring_position(member, n):
    return jnp.where(member % 2 == 0, member // 2, n - 1 - member // 2)


def ring_member(position, n):
    position = lax.rem(position + 2 * n, n)
    return jnp.where(position < n // 2, 2 * position, 2 * (n - 1 - position) + 1)


def swap_pairs(x):
    lane = lax.broadcasted_iota(jnp.int32, x.shape, 1)
    width = x.shape[1]
    return jnp.where(lane % 2 == 0, pltpu.roll(x, width - 1, 1), pltpu.roll(x, 1, 1))


def layer_kernel(
    n, chunks, pieces, arriving, gain_hbm, wq, wk, wv, w_hbm, tables_hbm,
    attended_ref, stream_ref,
    staged, gain, tables, x_all, weights, acc, squares, sent, got, heads_kv, key_head, value_head, q_ref, w_out, context, running,
    stage_sem, gain_sem, tables_sem, w_sem, wo_sem, shift_send, shift_recv, ring_send, ring_recv, kv_send, kv_recv, send_sem, recv_sem,
):
    sections = lax.axis_size("section")
    section = lax.axis_index("section")
    me = lax.axis_index("mp")
    position = ring_position(me, n)
    right, left = ring_member(position + 1, n), ring_member(position - 1, n)
    following, previous = lax.rem(section + 1, sections), lax.rem(section + sections - 1, sections)
    hops = n // 2
    per = n // chunks
    rows, width = x_all.shape[2:]
    length = n * rows
    chunk_rows = per * rows
    qw, kw, vw = wq.shape[0], wk.shape[0], wv.shape[0]
    heads = qw // HD
    group_size = heads * n // KV_HEADS
    nn = (((1,), (0,)), ((), ()))
    nt = (((1,), (1,)), ((), ()))

    stage = pltpu.make_async_copy(arriving, staged, stage_sem)
    stage.start()
    gain_copy = pltpu.make_async_copy(gain_hbm, gain, gain_sem)
    gain_copy.start()
    tables_copy = pltpu.make_async_copy(tables_hbm, tables, tables_sem)
    tables_copy.start()
    barrier = pltpu.get_barrier_semaphore()
    for step in range(1, n):
        pl.semaphore_signal(barrier, inc=1, device_id={"mp": lax.rem(me + step, n)}, device_id_type=MESH)
    for partner in (following, previous):
        pl.semaphore_signal(barrier, inc=1, device_id={"section": partner}, device_id_type=MESH)

    def weight_copy(j, part):
        src, start, size = ((wq, 0, qw), (wk, qw, kw), (wv, qw + kw, vw))[part]
        return pltpu.make_async_copy(
            src.at[:, pl.ds(j * width, width)], weights.at[j, pl.ds(start, size)], w_sem.at[j, part]
        )

    def shift_copy(c):
        return pltpu.make_async_remote_copy(
            src_ref=staged.at[pl.ds(c * per, per)],
            dst_ref=x_all.at[me, pl.ds(c * per, per)],
            send_sem=shift_send.at[c], recv_sem=shift_recv.at[c],
            device_id={"section": following}, device_id_type=MESH,
        )

    def ring_copy(way, hop, c):
        origin = ring_member(position - (hop - 1) if way == 0 else position + (hop - 1), n)
        return pltpu.make_async_remote_copy(
            src_ref=x_all.at[origin, pl.ds(c * per, per)],
            dst_ref=x_all.at[origin, pl.ds(c * per, per)],
            send_sem=ring_send.at[way, hop - 1, c], recv_sem=ring_recv.at[way, hop - 1, c],
            device_id={"mp": right if way == 0 else left}, device_id_type=MESH,
        )

    for j in range(n):
        for part in range(3):
            weight_copy(j, part).start()
    stage.wait()
    pl.semaphore_wait(barrier, n + 1)
    for c in range(chunks):
        shift_copy(c).start()
    acc[...] = jnp.zeros_like(acc)
    squares[...] = jnp.zeros_like(squares)

    def compute(slot, c):
        x = x_all[slot, pl.ds(c * per, per)].astype(jnp.float32).reshape(chunk_rows, width)
        total = x[:, :128] * x[:, :128]
        for g in range(1, width // 128):
            part = x[:, g * 128 : (g + 1) * 128]
            total = total + part * part
        squares[c] += total
        scaled = (x * gain[slot].astype(jnp.float32)).astype(jnp.bfloat16)
        acc[c] += lax.dot_general(scaled, weights[slot], nt, preferred_element_type=jnp.float32)

    for c in range(chunks):
        shift_copy(c).wait_recv()
        ring_copy(0, 1, c).start()
        ring_copy(1, 1, c).start()
    for j in range(n):
        for part in range(3):
            weight_copy(j, part).wait()
    gain_copy.wait()
    tables_copy.wait()
    wo_copy = pltpu.make_async_copy(w_hbm, w_out, wo_sem)
    wo_copy.start()

    @pl.loop(0, chunks)
    def _(c):
        compute(me, c)

    cos, sin = tables[0], tables[1]
    lane = lax.broadcasted_iota(jnp.int32, (HD, kw), 1)
    source = lax.broadcasted_iota(jnp.int32, (HD, kw), 0)
    pick = (source == (me * kw + lane) // (2 * KV_HEADS) * 2 + lane % 2).astype(jnp.float32)
    k_cos = lax.dot_general(cos, pick, nn, precision=lax.Precision.HIGHEST, preferred_element_type=jnp.float32)
    k_sin = lax.dot_general(sin, pick, nn, precision=lax.Precision.HIGHEST, preferred_element_type=jnp.float32)
    per_head = kw // KV_HEADS
    target = lax.broadcasted_iota(jnp.int32, (kw, kw), 0)
    origin_row = lax.broadcasted_iota(jnp.int32, (kw, kw), 1)
    head, within = target // per_head, target % per_head
    order = (origin_row == (within // 2 * KV_HEADS + head) * 2 + within % 2).astype(jnp.bfloat16)

    @pl.loop(0, hops * chunks)
    def _(i):
        hop = i // chunks + 1
        turn = lax.rem(i, chunks)
        last = hop == hops
        c = jnp.where(last, turn // 2 + lax.rem(turn, 2) * (chunks // 2), turn)
        low = c < chunks // 2
        for way in range(2):
            mine = low if way == 0 else jnp.logical_not(low)

            @pl.when(jnp.logical_or(jnp.logical_not(last), mine))
            def _():
                ring_copy(way, hop, c).wait_recv()

            @pl.when(jnp.logical_and(hop < hops, jnp.logical_or(hop + 1 < hops, mine)))
            def _():
                ring_copy(way, hop + 1, c).start()

        @pl.loop(0, 2)
        def _(way):
            mine = low == (way == 0)

            @pl.when(jnp.logical_or(jnp.logical_not(last), mine))
            def _():
                compute(ring_member(jnp.where(way == 0, position - hop, position + hop), n), c)

    inverse = lax.rsqrt(
        jnp.sum(squares[...].reshape(length, 128), axis=1, keepdims=True) * (1.0 / (n * width)) + NORM_EPS
    )
    k = acc[:, :, qw : qw + kw].reshape(length, kw) * inverse
    k_rot = (k * k_cos + swap_pairs(k) * k_sin).astype(jnp.bfloat16)
    def kv_copy(part, step):
        other = lax.rem(me + step, n)
        return pltpu.make_async_remote_copy(
            src_ref=sent.at[other * heads // group_size, part], dst_ref=got.at[me, part],
            send_sem=kv_send.at[part, step - 1], recv_sem=kv_recv.at[part, step - 1],
            device_id={"mp": other}, device_id_type=MESH,
        )

    def order_and_send(part, channels):
        ordered = lax.dot_general(order, channels, nt, preferred_element_type=jnp.float32)
        for h in range(KV_HEADS):
            sent[h, part] = ordered[h * per_head : (h + 1) * per_head].astype(jnp.bfloat16)
        for step in range(1, n):
            kv_copy(part, step).start()

    order_and_send(0, k_rot)
    order_and_send(1, (acc[:, :, qw + kw :].reshape(length, vw) * inverse).astype(jnp.bfloat16))
    got[me] = sent[me * heads // group_size]
    for h in range(heads):
        q = acc[:, :, h * HD : (h + 1) * HD].reshape(length, HD) * inverse
        q_ref[:, :, h * HD : (h + 1) * HD] = (
            (q * cos + swap_pairs(q) * sin).reshape(n, rows, HD).astype(jnp.bfloat16)
        )

    def receive(part, whole):
        for step in range(1, n):
            kv_copy(part, step).wait_recv()
        for j in range(n):
            heads_kv[part, j * per_head : (j + 1) * per_head] = got[j, part].astype(jnp.float32)
        whole[...] = heads_kv[part].astype(jnp.bfloat16)

    receive(0, key_head)

    piece_width = running.shape[4]
    scale = 1.0 / math.sqrt(HD)

    def attend(block, ready=None):
        row = lax.broadcasted_iota(jnp.int32, (rows, length), 0) + block * rows
        column = lax.broadcasted_iota(jnp.int32, (rows, length), 1)
        probs = []
        for h in range(heads):
            q = q_ref[block, :, h * HD : (h + 1) * HD]
            scores = lax.dot_general(q, key_head[...], nn, preferred_element_type=jnp.float32) * scale
            scores = jnp.where(row >= column, scores, -1e30)
            exponent = jnp.exp(scores - jnp.max(scores, axis=1, keepdims=True))
            probs.append((exponent / jnp.sum(exponent, axis=1, keepdims=True)).astype(jnp.bfloat16))
        if ready is not None:
            ready()
        for h in range(heads):
            context[block, :, h * HD : (h + 1) * HD] = lax.dot_general(
                probs[h], value_head[...], nt, preferred_element_type=jnp.float32
            ).astype(jnp.bfloat16)

    def block_of(way, step):
        return ring_member(position - 1 - step if way == 0 else position + 1 + step, n)

    def term(way, step, piece):
        start = (way * pieces + piece) * piece_width
        return jnp.dot(
            context[block_of(way, step)], w_out[:, start : start + piece_width], preferred_element_type=jnp.float32
        )

    def sum_copy(way, step, piece):
        return pltpu.make_async_remote_copy(
            src_ref=running.at[way, step, piece],
            dst_ref=running.at[way, step + 1, piece],
            send_sem=send_sem.at[way, step, piece], recv_sem=recv_sem.at[way, step, piece],
            device_id={"mp": right if way == 0 else left}, device_id_type=MESH,
        )

    wo_copy.wait()
    for way in range(2):
        attend(block_of(way, 0), functools.partial(receive, 1, value_head) if way == 0 else None)
        for piece in range(pieces):
            running[way, 0, piece] = term(way, 0, piece).astype(jnp.bfloat16)
            sum_copy(way, 0, piece).start()

    def ahead(step):
        @pl.when(step < n // 2)
        def _():
            attend(block_of(0, step))
            attend(block_of(1, step))

        @pl.when(step == n // 2)
        def _():
            attend(me)

    ahead(1)

    @pl.loop(1, n - 1)
    def _(step):
        for piece in range(pieces):
            for way in range(2):
                value = term(way, step, piece)
                sum_copy(way, step - 1, piece).wait_recv()
                running[way, step, piece] = (running[way, step, piece].astype(jnp.float32) + value).astype(jnp.bfloat16)
                sum_copy(way, step, piece).start()
        ahead(step + 1)

    for j in range(n):
        stream_ref[:, j * width : (j + 1) * width] = x_all[j, me]
    for piece in range(pieces):
        for way in range(2):
            value = term(way, n - 1, piece)
            sum_copy(way, n - 2, piece).wait_recv()
            value = running[way, n - 1, piece].astype(jnp.float32) + value
            columns = slice((way * pieces + piece) * piece_width, (way * pieces + piece + 1) * piece_width)
            attended_ref[:, columns] = value.astype(jnp.bfloat16)
            stream_ref[:, columns] = (stream_ref[:, columns].astype(jnp.float32) + value).astype(jnp.bfloat16)

    for c in range(chunks):
        shift_copy(c).wait_send()
    for part in range(2):
        for step in range(1, n):
            kv_copy(part, step).wait_send()

    @pl.loop(0, hops * chunks)
    def _(i):
        hop = i // chunks + 1
        c = lax.rem(i, chunks)
        for way in range(2):
            mine = (c < chunks // 2) if way == 0 else (c >= chunks // 2)

            @pl.when(jnp.logical_or(hop < hops, mine))
            def _():
                ring_copy(way, hop, c).wait_send()

    @pl.loop(0, n - 1)
    def _(step):
        for piece in range(pieces):
            for way in range(2):
                sum_copy(way, step, piece).wait_send()


def rotary_tables(length):
    pair = (np.arange(HD) // 2).astype(np.float32)
    frequency = np.exp(pair * np.float32(-2.0 * math.log(ROPE_BASE) / HD)).astype(np.float32)
    angles = frequency[None, :] * np.arange(length, dtype=np.float32)[:, None]
    sign = np.where(np.arange(HD) % 2 == 0, -1.0, 1.0).astype(np.float32)
    return np.stack([np.cos(angles), np.sin(angles) * sign]).astype(np.float32)


def local(arriving, norm_gain, w_query, w_key, w_value, w_out):
    n = lax.axis_size("mp")
    length, width = arriving.shape[1:]
    rows = length // n
    full = n * width
    chunks = 8 if n <= 8 else 2
    pieces = 4 if n <= 8 else 2
    qw, kw, vw = w_query.shape[1], w_key.shape[1], w_value.shape[1]
    tables = rotary_tables(length)
    vmem = pl.BlockSpec(memory_space=pltpu.VMEM)
    hbm = pl.BlockSpec(memory_space=pltpu.HBM)
    bf16, f32 = jnp.bfloat16, jnp.float32
    dma = pltpu.SemaphoreType.DMA
    attended, stream = pl.pallas_call(
        functools.partial(layer_kernel, n, chunks, pieces),
        name="layer",
        out_shape=(pltpu.VMEM((rows, full), bf16),) * 2,
        in_specs=[hbm] * 7,
        out_specs=(vmem, vmem),
        scratch_shapes=[
            pltpu.VMEM((n, rows, width), bf16),
            pltpu.VMEM((n, 1, width), bf16),
            pltpu.VMEM((2, length, HD), f32),
            pltpu.VMEM((n, n, rows, width), bf16),
            pltpu.VMEM((n, qw + kw + vw, width), bf16),
            pltpu.VMEM((chunks, length // chunks, qw + kw + vw), f32),
            pltpu.VMEM((chunks, length // chunks, 128), f32),
            pltpu.VMEM((KV_HEADS, 2, kw // KV_HEADS, length), bf16),
            pltpu.VMEM((n, 2, kw // KV_HEADS, length), bf16),
            pltpu.VMEM((2, HD, length), f32),
            pltpu.VMEM((HD, length), bf16),
            pltpu.VMEM((HD, length), bf16),
            pltpu.VMEM((n, rows, qw), bf16),
            pltpu.VMEM((qw, full), bf16),
            pltpu.VMEM((n, rows, qw), bf16),
            pltpu.VMEM((2, n, pieces, rows, full // (2 * pieces)), bf16),
            dma(()),
            dma(()),
            dma(()),
            dma((n, 3)),
            dma(()),
            dma((chunks,)),
            dma((chunks,)),
            dma((2, n // 2, chunks)),
            dma((2, n // 2, chunks)),
            dma((2, n - 1)),
            dma((2, n - 1)),
            dma((2, n - 1, pieces)),
            dma((2, n - 1, pieces)),
        ],
        compiler_params=pltpu.CompilerParams(collective_id=0, has_side_effects=True, vmem_limit_bytes=VMEM_LIMIT),
    )(
        arriving[0].reshape(n, rows, width),
        norm_gain[0].reshape(n, 1, width),
        w_query[0], w_key[0], w_value[0], w_out[0], jnp.asarray(tables),
    )
    return (attended[None], stream[None])


def solution(mesh):
    return jax.shard_map(
        local,
        mesh=mesh,
        in_specs=(
            P("section", None, "mp"),
            P("section", None),
            P("section", "mp", None),
            P("section", "mp", None),
            P("section", "mp", None),
            P("section", "mp", None),
        ),
        out_specs=(P("section", "mp", None), P("section", "mp", None)),
        check_vma=False,
    )
```

profile of v0, /device:TPU:4, one launch (start us, length us, event | category | flops | bytes accessed | tf_op | source)
XLA Modules:
  0.0 262.2 jit_solution(3461691908761710543)
XLA Ops:
  0.6 259.2 %layer.1 = (bf16[96,8192]{1,0:T(8,128)(2,1)S(1)}, bf16[96,8192]{1,0:T(8,128)(2,1)S(1)}) custom-call(bf16[8,96,1024]{2,1,0:T(8,128)(2,1)} %bitcast.14, bf16[8,1,1024]{2,1,0:T(2,128)(2,1)} %bitcast.15, bf16[256,8192]{1,0:T(8,128)(2,1)} %bitcast.10, bf16[128,8192]{1,0:T(8,128)(2,1)} %bitcast.12, bf16[128,8192]{1,0:T(8,128)(2,1)} %bitcast.13, ...), custom_call_target="tpu_custom_call" | custom-call | tf_op jit(solution)/shard_map/layer/pallas_call | solution.py:327
  259.9 1.1 copy.11
  261.0 1.1 copy.12
where the time goes:
time: 262 us
  Pallas kernels  259 us (99%)
    pallas_call x1, Pallas kernels, local(): pl.pallas_call(functools.partial(layer_kernel, n, chunks, pieces), name='...  259 us

commit v1 on v0

--- a/solution.py
+++ b/solution.py
@@ -15,6 +15,9 @@
 NORM_EPS = 1e-05
 MESH = pl.DeviceIdType.MESH
 VMEM_LIMIT = 63500000
+EARLY = 9
+LATE = 2
+LEAD = 4
 
 
 def ring_position(member, n):
@@ -32,7 +35,7 @@
     return jnp.where(lane % 2 == 0, pltpu.roll(x, width - 1, 1), pltpu.roll(x, 1, 1))
 
 
-def layer_kernel(
+def ring_kernel(
     n, chunks, pieces, arriving, gain_hbm, wq, wk, wv, w_hbm, tables_hbm,
     attended_ref, stream_ref,
     staged, gain, tables, x_all, weights, acc, squares, sent, got, heads_kv, key_head, value_head, q_ref, w_out, context, running,
@@ -303,6 +306,441 @@
                 sum_copy(way, step, piece).wait_send()
 
 
+def grid_kernel(
+    n, chunks, pieces, arriving, gain_hbm, wq, wk, wv, w_hbm, tables_hbm,
+    attended_ref, stream_ref,
+    staged, gain, tables, x_all, weights, acc, squares, sent, got, heads_kv, key_head, value_head, q_ref,
+    context, w_half, leaving, entering, summed, final,
+    stage_sem, gain_sem, tables_sem, w_sem, shift_send, shift_recv, ring_send, ring_recv, short_send, kv_send, kv_recv,
+    wo_own, wo_send, wo_recv, context_send, context_recv, mid_send, mid_recv, final_send, final_recv,
+):
+    sections = lax.axis_size("section")
+    section = lax.axis_index("section")
+    me = lax.axis_index("mp")
+    position = ring_position(me, n)
+    right, left = ring_member(position + 1, n), ring_member(position - 1, n)
+    following, previous = lax.rem(section + 1, sections), lax.rem(section + sections - 1, sections)
+    hops = n // 2
+    per = n // chunks
+    rows, width = x_all.shape[2:]
+    length = n * rows
+    chunk_rows = per * rows
+    qw, kw, vw = wq.shape[0], wk.shape[0], wv.shape[0]
+    heads = qw // HD
+    group_size = heads * n // KV_HEADS
+    nn = (((1,), (0,)), ((), ()))
+    nt = (((1,), (1,)), ((), ()))
+
+    z, x = me // 2, lax.rem(me, 2)
+    half = z // 2
+    inner_row = 1 + half
+    inner = z == inner_row
+    corner = jnp.logical_not(inner)
+    out_way = lax.rem(position, 2)
+    partner = 2 * z + 1 - x
+    opposite = 2 * (2 - half) + x
+    beyond = ring_member(jnp.where(out_way == 1, position + 1, position - 1), n)
+    slot = jnp.where(inner, 2, 0) + x
+    per_half = n // 2
+    half_first = half * per_half
+
+    stage = pltpu.make_async_copy(arriving, staged, stage_sem)
+    stage.start()
+    gain_copy = pltpu.make_async_copy(gain_hbm, gain, gain_sem)
+    gain_copy.start()
+    tables_copy = pltpu.make_async_copy(tables_hbm, tables, tables_sem)
+    tables_copy.start()
+    barrier = pltpu.get_barrier_semaphore()
+    for step in range(1, n):
+        pl.semaphore_signal(barrier, inc=1, device_id={"mp": lax.rem(me + step, n)}, device_id_type=MESH)
+    for partner_section in (following, previous):
+        pl.semaphore_signal(barrier, inc=1, device_id={"section": partner_section}, device_id_type=MESH)
+
+    def weight_copy(j, part):
+        src, start, size = ((wq, 0, qw), (wk, qw, kw), (wv, qw + kw, vw))[part]
+        return pltpu.make_async_copy(
+            src.at[:, pl.ds(j * width, width)], weights.at[j, pl.ds(start, size)], w_sem.at[j, part]
+        )
+
+    def shift_copy(c):
+        return pltpu.make_async_remote_copy(
+            src_ref=staged.at[pl.ds(c * per, per)],
+            dst_ref=x_all.at[me, pl.ds(c * per, per)],
+            send_sem=shift_send.at[c], recv_sem=shift_recv.at[c],
+            device_id={"section": following}, device_id_type=MESH,
+        )
+
+    def ring_copy(way, hop, c):
+        origin = ring_member(position - (hop - 1) if way == 0 else position + (hop - 1), n)
+        return pltpu.make_async_remote_copy(
+            src_ref=x_all.at[origin, pl.ds(c * per, per)],
+            dst_ref=x_all.at[origin, pl.ds(c * per, per)],
+            send_sem=ring_send.at[way, hop - 1, c], recv_sem=ring_recv.at[way, hop - 1, c],
+            device_id={"mp": right if way == 0 else left}, device_id_type=MESH,
+        )
+
+    def short_copy(late, c):
+        origin = beyond if late else me
+        return pltpu.make_async_remote_copy(
+            src_ref=x_all.at[origin, pl.ds(c * per, per)],
+            dst_ref=x_all.at[origin, pl.ds(c * per, per)],
+            send_sem=short_send.at[late, c], recv_sem=ring_recv.at[out_way, hops - 2 + late, c],
+            device_id={"mp": partner}, device_id_type=MESH,
+        )
+
+    def low_or_high(way, c):
+        return c < chunks // 2 if way == 0 else c >= chunks // 2
+
+    def sends(way, hop, c):
+        on = jnp.logical_not(jnp.logical_and(jnp.logical_and(corner, out_way == way), hop >= hops - 1))
+        return jnp.logical_and(on, jnp.logical_or(hop < hops, low_or_high(way, c)))
+
+    piece_width = w_half.shape[3]
+
+    def wo_source(target, k):
+        owner = jnp.where(target == 0, x, 1 - x)
+        start = pl.multiple_of(owner * (pieces * piece_width) + k * piece_width, piece_width)
+        return w_hbm.at[:, pl.ds(start, piece_width)], 2 * inner_row + owner
+
+    def wo_copy(target, k):
+        src, device = wo_source(target, k)
+        return pltpu.make_async_remote_copy(
+            src_ref=src, dst_ref=w_half.at[k, slot],
+            send_sem=wo_send.at[target, k], recv_sem=wo_recv.at[slot, k],
+            device_id={"mp": device}, device_id_type=MESH,
+        )
+
+    def wo_own_copy(k):
+        src, _ = wo_source(0, k)
+        return pltpu.make_async_copy(src, w_half.at[k, slot], wo_own.at[k])
+
+    def wo_arrived(s, k):
+        return pltpu.make_async_remote_copy(
+            src_ref=w_half.at[k, s], dst_ref=w_half.at[k, s],
+            send_sem=wo_send.at[0, k], recv_sem=wo_recv.at[s, k],
+            device_id={"mp": partner}, device_id_type=MESH,
+        )
+
+    for j in range(n):
+        for part in range(3):
+            weight_copy(j, part).start()
+    stage.wait()
+    pl.semaphore_wait(barrier, n + 1)
+    for c in range(chunks):
+        shift_copy(c).start()
+    acc[...] = jnp.zeros_like(acc)
+    squares[...] = jnp.zeros_like(squares)
+
+    def compute(source, c):
+        block = x_all[source, pl.ds(c * per, per)].astype(jnp.float32).reshape(chunk_rows, width)
+        total = block[:, :128] * block[:, :128]
+        for g in range(1, width // 128):
+            part = block[:, g * 128 : (g + 1) * 128]
+            total = total + part * part
+        squares[c] += total
+        scaled = (block * gain[source].astype(jnp.float32)).astype(jnp.bfloat16)
+        acc[c] += lax.dot_general(scaled, weights[source], nt, preferred_element_type=jnp.float32)
+
+    for c in range(chunks):
+        shift_copy(c).wait_recv()
+        ring_copy(0, 1, c).start()
+        ring_copy(1, 1, c).start()
+
+        @pl.when(inner)
+        def _():
+            short_copy(0, c).start()
+    for j in range(n):
+        for part in range(3):
+            weight_copy(j, part).wait()
+    gain_copy.wait()
+    tables_copy.wait()
+
+    @pl.when(inner)
+    def _():
+        @pl.loop(0, pieces)
+        def _(k):
+            wo_own_copy(k).start()
+
+    @pl.loop(0, chunks)
+    def _(c):
+        compute(me, c)
+
+    cos, sin = tables[0], tables[1]
+    lane = lax.broadcasted_iota(jnp.int32, (HD, kw), 1)
+    source = lax.broadcasted_iota(jnp.int32, (HD, kw), 0)
+    pick = (source == (me * kw + lane) // (2 * KV_HEADS) * 2 + lane % 2).astype(jnp.float32)
+    k_cos = lax.dot_general(cos, pick, nn, precision=lax.Precision.HIGHEST, preferred_element_type=jnp.float32)
+    k_sin = lax.dot_general(sin, pick, nn, precision=lax.Precision.HIGHEST, preferred_element_type=jnp.float32)
+    per_head = kw // KV_HEADS
+    target = lax.broadcasted_iota(jnp.int32, (kw, kw), 0)
+    origin_row = lax.broadcasted_iota(jnp.int32, (kw, kw), 1)
+    head, within = target // per_head, target % per_head
+    order = (origin_row == (within // 2 * KV_HEADS + head) * 2 + within % 2).astype(jnp.bfloat16)
+
+    @pl.loop(0, hops * chunks)
+    def _(i):
+        hop = i // chunks + 1
+        turn = lax.rem(i, chunks)
+        last = hop == hops
+        c = jnp.where(last, turn // 2 + lax.rem(turn, 2) * (chunks // 2), turn)
+        low = c < chunks // 2
+        for way in range(2):
+            mine = low_or_high(way, c)
+
+            @pl.when(jnp.logical_or(jnp.logical_not(last), mine))
+            def _():
+                ring_copy(way, hop, c).wait_recv()
+
+            @pl.when(jnp.logical_and(hop < hops, sends(way, hop + 1, c)))
+            def _():
+                ring_copy(way, hop + 1, c).start()
+
+            @pl.when(jnp.logical_and(jnp.logical_and(inner, out_way == way), jnp.logical_and(hop == 1, mine)))
+            def _():
+                short_copy(1, c).start()
+
+        @pl.when(jnp.logical_and(inner, hop == hops - 2))
+        def _():
+            wo_copy(1, turn).start()
+
+        early = i - (hops - 3) * chunks
+
+        @pl.when(jnp.logical_and(corner, jnp.logical_and(early >= 0, early < EARLY)))
+        def _():
+            wo_copy(lax.rem(early, 2), early // 2).start()
+
+        @pl.loop(0, 2)
+        def _(way):
+            mine = low == (way == 0)
+
+            @pl.when(jnp.logical_or(jnp.logical_not(last), mine))
+            def _():
+                compute(ring_member(jnp.where(way == 0, position - hop, position + hop), n), c)
+
+    inverse = lax.rsqrt(
+        jnp.sum(squares[...].reshape(length, 128), axis=1, keepdims=True) * (1.0 / (n * width)) + NORM_EPS
+    )
+    k = acc[:, :, qw : qw + kw].reshape(length, kw) * inverse
+    k_rot = (k * k_cos + swap_pairs(k) * k_sin).astype(jnp.bfloat16)
+
+    def kv_copy(part, step):
+        other = lax.rem(me + step, n)
+        return pltpu.make_async_remote_copy(
+            src_ref=sent.at[other * heads // group_size, part], dst_ref=got.at[me, part],
+            send_sem=kv_send.at[part, step - 1], recv_sem=kv_recv.at[part, step - 1],
+            device_id={"mp": other}, device_id_type=MESH,
+        )
+
+    def order_and_send(part, channels):
+        ordered = lax.dot_general(order, channels, nt, preferred_element_type=jnp.float32)
+        for h in range(KV_HEADS):
+            sent[h, part] = ordered[h * per_head : (h + 1) * per_head].astype(jnp.bfloat16)
+        for step in range(1, n):
+            kv_copy(part, step).start()
+
+    order_and_send(0, k_rot)
+    order_and_send(1, (acc[:, :, qw + kw :].reshape(length, vw) * inverse).astype(jnp.bfloat16))
+    got[me] = sent[me * heads // group_size]
+    for h in range(heads):
+        q = acc[:, :, h * HD : (h + 1) * HD].reshape(length, HD) * inverse
+        q_ref[:, :, h * HD : (h + 1) * HD] = (
+            (q * cos + swap_pairs(q) * sin).reshape(n, rows, HD).astype(jnp.bfloat16)
+        )
+
+    def receive(part, whole):
+        for step in range(1, n):
+            kv_copy(part, step).wait_recv()
+        for j in range(n):
+            heads_kv[part, j * per_head : (j + 1) * per_head] = got[j, part].astype(jnp.float32)
+        whole[...] = heads_kv[part].astype(jnp.bfloat16)
+
+    receive(0, key_head)
+    receive(1, value_head)
+
+    scale = 1.0 / math.sqrt(HD)
+
+    def attend(block):
+        row = lax.broadcasted_iota(jnp.int32, (rows, length), 0) + block * rows
+        column = lax.broadcasted_iota(jnp.int32, (rows, length), 1)
+        for h in range(heads):
+            q = q_ref[block, :, h * HD : (h + 1) * HD]
+            scores = lax.dot_general(q, key_head[...], nn, preferred_element_type=jnp.float32) * scale
+            scores = jnp.where(row >= column, scores, -1e30)
+            exponent = jnp.exp(scores - jnp.max(scores, axis=1, keepdims=True))
+            probs = (exponent / jnp.sum(exponent, axis=1, keepdims=True)).astype(jnp.bfloat16)
+            context[slot, block, :, h * HD : (h + 1) * HD] = lax.dot_general(
+                probs, value_head[...], nt, preferred_element_type=jnp.float32
+            ).astype(jnp.bfloat16)
+
+    def context_copy(target, block):
+        return pltpu.make_async_remote_copy(
+            src_ref=context.at[slot, block], dst_ref=context.at[slot, block],
+            send_sem=context_send.at[target, block], recv_sem=context_recv.at[slot, block],
+            device_id={"mp": 2 * inner_row + (x if target == 0 else 1 - x)}, device_id_type=MESH,
+        )
+
+    def context_arrived(s, block):
+        return pltpu.make_async_remote_copy(
+            src_ref=context.at[s, block], dst_ref=context.at[s, block],
+            send_sem=context_send.at[0, block], recv_sem=context_recv.at[s, block],
+            device_id={"mp": partner}, device_id_type=MESH,
+        )
+
+    @pl.loop(0, n)
+    def _(i):
+        block = lax.rem(per_half - half_first + i, n)
+        attend(block)
+
+        @pl.when(corner)
+        def _():
+            context_copy(0, block).start()
+
+        context_copy(1, block).start()
+
+        @pl.when(jnp.logical_and(corner, i >= per_half - 1))
+        def _():
+            first = EARLY + (i - (per_half - 1)) * LATE
+
+            @pl.loop(first, jnp.minimum(first + LATE, 2 * pieces))
+            def _(late):
+                wo_copy(lax.rem(late, 2), late // 2).start()
+
+    slots = context.shape[0]
+
+    def term(first, k):
+        total = jnp.zeros((per_half * rows, piece_width), jnp.float32)
+        for s in range(slots):
+            total += jnp.dot(
+                context[s, pl.ds(first, per_half)].reshape(per_half * rows, qw), w_half[k, s],
+                preferred_element_type=jnp.float32,
+            )
+        return total
+
+    def mid_copy(k):
+        return pltpu.make_async_remote_copy(
+            src_ref=leaving.at[k], dst_ref=entering.at[k],
+            send_sem=mid_send.at[k], recv_sem=mid_recv.at[k],
+            device_id={"mp": opposite}, device_id_type=MESH,
+        )
+
+    def final_copy(k, b):
+        return pltpu.make_async_remote_copy(
+            src_ref=summed.at[k, b], dst_ref=final.at[x, k],
+            send_sem=final_send.at[k, b], recv_sem=final_recv.at[x, k],
+            device_id={"mp": half_first + b}, device_id_type=MESH,
+        )
+
+    def final_arrived(side, k):
+        return pltpu.make_async_remote_copy(
+            src_ref=final.at[side, k], dst_ref=final.at[side, k],
+            send_sem=final_send.at[k, 0], recv_sem=final_recv.at[side, k],
+            device_id={"mp": partner}, device_id_type=MESH,
+        )
+
+    def contexts_arrived(first):
+        for s in range(slots):
+            @pl.when(slot != s)
+            def _():
+                @pl.loop(0, per_half)
+                def _(b):
+                    context_arrived(s, first + b).wait_recv()
+
+    @pl.when(inner)
+    def _():
+        contexts_arrived(per_half - half_first)
+
+        @pl.loop(0, pieces + LEAD)
+        def _(i):
+            @pl.when(i < pieces)
+            def _():
+                wo_own_copy(i).wait()
+                for s in range(slots):
+                    @pl.when(slot != s)
+                    def _():
+                        wo_arrived(s, i).wait_recv()
+                leaving[i] = term(per_half - half_first, i).astype(jnp.bfloat16)
+                mid_copy(i).start()
+
+            @pl.when(i == LEAD)
+            def _():
+                contexts_arrived(half_first)
+
+            @pl.when(i >= LEAD)
+            def _():
+                k = i - LEAD
+                value = term(half_first, k)
+                mid_copy(k).wait_recv()
+                value = value + entering[k].astype(jnp.float32)
+                summed[k] = value.astype(jnp.bfloat16).reshape(per_half, rows, piece_width)
+                for b in range(per_half):
+                    @pl.when(half_first + b != me)
+                    def _():
+                        final_copy(k, b).start()
+                final[x, k] = summed[k, me - half_first]
+
+    @pl.loop(0, pieces)
+    def _(k):
+        for side in range(2):
+            @pl.when(jnp.logical_or(corner, x != side))
+            def _():
+                final_arrived(side, k).wait_recv()
+            start = side * (pieces * piece_width) + k * piece_width
+            columns = pl.ds(pl.multiple_of(start, piece_width), piece_width)
+            within_block = pl.ds(pl.multiple_of(lax.rem(start, width), piece_width), piece_width)
+            value = final[side, k]
+            attended_ref[:, columns] = value
+            stream_ref[:, columns] = (
+                x_all[start // width, me, :, within_block].astype(jnp.float32) + value.astype(jnp.float32)
+            ).astype(jnp.bfloat16)
+
+    for c in range(chunks):
+        shift_copy(c).wait_send()
+    for part in range(2):
+        for step in range(1, n):
+            kv_copy(part, step).wait_send()
+
+    @pl.loop(0, hops * chunks)
+    def _(i):
+        hop = i // chunks + 1
+        c = lax.rem(i, chunks)
+        for way in range(2):
+            @pl.when(sends(way, hop, c))
+            def _():
+                ring_copy(way, hop, c).wait_send()
+
+    @pl.loop(0, n)
+    def _(block):
+        @pl.when(corner)
+        def _():
+            context_copy(0, block).wait_send()
+        context_copy(1, block).wait_send()
+
+    @pl.loop(0, pieces)
+    def _(k):
+        wo_copy(1, k).wait_send()
+
+        @pl.when(corner)
+        def _():
+            wo_copy(0, k).wait_send()
+
+        @pl.when(inner)
+        def _():
+            mid_copy(k).wait_send()
+            for b in range(per_half):
+                @pl.when(half_first + b != me)
+                def _():
+                    final_copy(k, b).wait_send()
+
+    @pl.when(inner)
+    def _():
+        for c in range(chunks):
+            short_copy(0, c).wait_send()
+
+            @pl.when((c < chunks // 2) == (out_way == 0))
+            def _():
+                short_copy(1, c).wait_send()
+
+
 def rotary_tables(length):
     pair = (np.arange(HD) // 2).astype(np.float32)
     frequency = np.exp(pair * np.float32(-2.0 * math.log(ROPE_BASE) / HD)).astype(np.float32)
@@ -324,26 +762,61 @@
     hbm = pl.BlockSpec(memory_space=pltpu.HBM)
     bf16, f32 = jnp.bfloat16, jnp.float32
     dma = pltpu.SemaphoreType.DMA
-    attended, stream = pl.pallas_call(
-        functools.partial(layer_kernel, n, chunks, pieces),
-        name="layer",
-        out_shape=(pltpu.VMEM((rows, full), bf16),) * 2,
-        in_specs=[hbm] * 7,
-        out_specs=(vmem, vmem),
-        scratch_shapes=[
-            pltpu.VMEM((n, rows, width), bf16),
-            pltpu.VMEM((n, 1, width), bf16),
-            pltpu.VMEM((2, length, HD), f32),
-            pltpu.VMEM((n, n, rows, width), bf16),
-            pltpu.VMEM((n, qw + kw + vw, width), bf16),
-            pltpu.VMEM((chunks, length // chunks, qw + kw + vw), f32),
-            pltpu.VMEM((chunks, length // chunks, 128), f32),
-            pltpu.VMEM((KV_HEADS, 2, kw // KV_HEADS, length), bf16),
-            pltpu.VMEM((n, 2, kw // KV_HEADS, length), bf16),
-            pltpu.VMEM((2, HD, length), f32),
-            pltpu.VMEM((HD, length), bf16),
-            pltpu.VMEM((HD, length), bf16),
-            pltpu.VMEM((n, rows, qw), bf16),
+    operands = (
+        arriving[0].reshape(n, rows, width),
+        norm_gain[0].reshape(n, 1, width),
+        w_query[0], w_key[0], w_value[0], w_out[0], jnp.asarray(tables),
+    )
+    shared = [
+        pltpu.VMEM((n, rows, width), bf16),
+        pltpu.VMEM((n, 1, width), bf16),
+        pltpu.VMEM((2, length, HD), f32),
+        pltpu.VMEM((n, n, rows, width), bf16),
+        pltpu.VMEM((n, qw + kw + vw, width), bf16),
+        pltpu.VMEM((chunks, length // chunks, qw + kw + vw), f32),
+        pltpu.VMEM((chunks, length // chunks, 128), f32),
+        pltpu.VMEM((KV_HEADS, 2, kw // KV_HEADS, length), bf16),
+        pltpu.VMEM((n, 2, kw // KV_HEADS, length), bf16),
+        pltpu.VMEM((2, HD, length), f32),
+        pltpu.VMEM((HD, length), bf16),
+        pltpu.VMEM((HD, length), bf16),
+        pltpu.VMEM((n, rows, qw), bf16),
+    ]
+    if n == 8:
+        pieces = 8
+        piece_width = full // (2 * pieces)
+        kernel = grid_kernel
+        scratch = shared + [
+            pltpu.VMEM((4, n, rows, qw), bf16),
+            pltpu.VMEM((pieces, 4, qw, piece_width), bf16),
+            pltpu.VMEM((pieces, length // 2, piece_width), bf16),
+            pltpu.VMEM((pieces, length // 2, piece_width), bf16),
+            pltpu.VMEM((pieces, n // 2, rows, piece_width), bf16),
+            pltpu.VMEM((2, pieces, rows, piece_width), bf16),
+            dma(()),
+            dma(()),
+            dma(()),
+            dma((n, 3)),
+            dma((chunks,)),
+            dma((chunks,)),
+            dma((2, n // 2, chunks)),
+            dma((2, n // 2, chunks)),
+            dma((2, chunks)),
+            dma((2, n - 1)),
+            dma((2, n - 1)),
+            dma((pieces,)),
+            dma((2, pieces)),
+            dma((4, pieces)),
+            dma((2, n)),
+            dma((4, n)),
+            dma((pieces,)),
+            dma((pieces,)),
+            dma((pieces, n // 2)),
+            dma((2, pieces)),
+        ]
+    else:
+        kernel = ring_kernel
+        scratch = shared + [
             pltpu.VMEM((qw, full), bf16),
             pltpu.VMEM((n, rows, qw), bf16),
             pltpu.VMEM((2, n, pieces, rows, full // (2 * pieces)), bf16),
@@ -360,13 +833,16 @@
             dma((2, n - 1)),
             dma((2, n - 1, pieces)),
             dma((2, n - 1, pieces)),
-        ],
+        ]
+    attended, stream = pl.pallas_call(
+        functools.partial(kernel, n, chunks, pieces),
+        name="layer",
+        out_shape=(pltpu.VMEM((rows, full), bf16),) * 2,
+        in_specs=[hbm] * 7,
+        out_specs=(vmem, vmem),
+        scratch_shapes=scratch,
         compiler_params=pltpu.CompilerParams(collective_id=0, has_side_effects=True, vmem_limit_bytes=VMEM_LIMIT),
-    )(
-        arriving[0].reshape(n, rows, width),
-        norm_gain[0].reshape(n, 1, width),
-        w_query[0], w_key[0], w_value[0], w_out[0], jnp.asarray(tables),
-    )
+    )(*operands)
     return (attended[None], stream[None])
 
 

time: 262 us -> 235 us (0.90)
  Pallas kernels: 259 us -> 231 us
    pallas_call x1, Pallas kernels: 259 us -> 231 us  [local(): pl.pallas_call(functools.partial(kernel, n, chunks, pieces), name='layer'...]
where the time goes in v1:
time: 235 us; the launch traced here: 234 us
  Pallas kernels  231 us (98%)
    pallas_call x1, Pallas kernels, local(): pl.pallas_call(functools.partial(kernel, n, chunks, pieces), name='layer'...  231 us

profile of v1, /device:TPU:4, one launch (start us, length us, event | category | flops | bytes accessed | tf_op | source)
XLA Modules:
  0.0 234.0 jit_solution(12488938693495918923)
XLA Ops:
  0.6 231.1 %layer.1 = (bf16[96,8192]{1,0:T(8,128)(2,1)S(1)}, bf16[96,8192]{1,0:T(8,128)(2,1)S(1)}) custom-call(bf16[8,96,1024]{2,1,0:T(8,128)(2,1)} %bitcast.14, bf16[8,1,1024]{2,1,0:T(2,128)(2,1)} %bitcast.15, bf16[256,8192]{1,0:T(8,128)(2,1)} %bitcast.10, bf16[128,8192]{1,0:T(8,128)(2,1)} %bitcast.12, bf16[128,8192]{1,0:T(8,128)(2,1)} %bitcast.13, ...), custom_call_target="tpu_custom_call" | custom-call | tf_op jit(solution)/shard_map/layer/pallas_call | solution.py:837
  231.7 1.1 copy.11
  232.9 1.1 copy.12

commit v2 on v1

--- a/solution.py
+++ b/solution.py
@@ -15,9 +15,9 @@
 NORM_EPS = 1e-05
 MESH = pl.DeviceIdType.MESH
 VMEM_LIMIT = 63500000
-EARLY = 9
-LATE = 2
-LEAD = 4
+AHEAD = 2
+LAG = 2
+LEAD = 3
 
 
 def ring_position(member, n):
@@ -309,7 +309,7 @@
 def grid_kernel(
     n, chunks, pieces, arriving, gain_hbm, wq, wk, wv, w_hbm, tables_hbm,
     attended_ref, stream_ref,
-    staged, gain, tables, x_all, weights, acc, squares, sent, got, heads_kv, key_head, value_head, q_ref,
+    staged, gain, tables, x_all, weights, acc, squares, rotary, sent, got, key_head, value_head, q_ref,
     context, w_half, leaving, entering, summed, final,
     stage_sem, gain_sem, tables_sem, w_sem, shift_send, shift_recv, ring_send, ring_recv, short_send, kv_send, kv_recv,
     wo_own, wo_send, wo_recv, context_send, context_recv, mid_send, mid_recv, final_send, final_recv,
@@ -321,15 +321,17 @@
     right, left = ring_member(position + 1, n), ring_member(position - 1, n)
     following, previous = lax.rem(section + 1, sections), lax.rem(section + sections - 1, sections)
     hops = n // 2
-    per = n // chunks
-    rows, width = x_all.shape[2:]
-    length = n * rows
-    chunk_rows = per * rows
+    rows = attended_ref.shape[0]
+    length, width = x_all.shape[1:]
+    per = length // chunks
     qw, kw, vw = wq.shape[0], wk.shape[0], wv.shape[0]
     heads = qw // HD
     group_size = heads * n // KV_HEADS
     nn = (((1,), (0,)), ((), ()))
     nt = (((1,), (1,)), ((), ()))
+
+    def part_of(c):
+        return pl.ds(pl.multiple_of(c * per, per), per)
 
     z, x = me // 2, lax.rem(me, 2)
     half = z // 2
@@ -364,8 +366,8 @@
 
     def shift_copy(c):
         return pltpu.make_async_remote_copy(
-            src_ref=staged.at[pl.ds(c * per, per)],
-            dst_ref=x_all.at[me, pl.ds(c * per, per)],
+            src_ref=staged.at[part_of(c)],
+            dst_ref=x_all.at[me, part_of(c)],
             send_sem=shift_send.at[c], recv_sem=shift_recv.at[c],
             device_id={"section": following}, device_id_type=MESH,
         )
@@ -373,8 +375,8 @@
     def ring_copy(way, hop, c):
         origin = ring_member(position - (hop - 1) if way == 0 else position + (hop - 1), n)
         return pltpu.make_async_remote_copy(
-            src_ref=x_all.at[origin, pl.ds(c * per, per)],
-            dst_ref=x_all.at[origin, pl.ds(c * per, per)],
+            src_ref=x_all.at[origin, part_of(c)],
+            dst_ref=x_all.at[origin, part_of(c)],
             send_sem=ring_send.at[way, hop - 1, c], recv_sem=ring_recv.at[way, hop - 1, c],
             device_id={"mp": right if way == 0 else left}, device_id_type=MESH,
         )
@@ -382,18 +384,18 @@
     def short_copy(late, c):
         origin = beyond if late else me
         return pltpu.make_async_remote_copy(
-            src_ref=x_all.at[origin, pl.ds(c * per, per)],
-            dst_ref=x_all.at[origin, pl.ds(c * per, per)],
+            src_ref=x_all.at[origin, part_of(c)],
+            dst_ref=x_all.at[origin, part_of(c)],
             send_sem=short_send.at[late, c], recv_sem=ring_recv.at[out_way, hops - 2 + late, c],
             device_id={"mp": partner}, device_id_type=MESH,
         )
 
-    def low_or_high(way, c):
-        return c < chunks // 2 if way == 0 else c >= chunks // 2
+    def own_parity(way, c):
+        return lax.rem(c, 2) == way
 
     def sends(way, hop, c):
         on = jnp.logical_not(jnp.logical_and(jnp.logical_and(corner, out_way == way), hop >= hops - 1))
-        return jnp.logical_and(on, jnp.logical_or(hop < hops, low_or_high(way, c)))
+        return jnp.logical_and(on, jnp.logical_or(hop < hops, own_parity(way, c)))
 
     piece_width = w_half.shape[3]
 
@@ -430,9 +432,11 @@
         shift_copy(c).start()
     acc[...] = jnp.zeros_like(acc)
     squares[...] = jnp.zeros_like(squares)
+    key_head[...] = jnp.zeros_like(key_head)
+    value_head[...] = jnp.zeros_like(value_head)
 
     def compute(source, c):
-        block = x_all[source, pl.ds(c * per, per)].astype(jnp.float32).reshape(chunk_rows, width)
+        block = x_all[source, part_of(c)].astype(jnp.float32)
         total = block[:, :128] * block[:, :128]
         for g in range(1, width // 128):
             part = block[:, g * 128 : (g + 1) * 128]
@@ -441,7 +445,7 @@
         scaled = (block * gain[source].astype(jnp.float32)).astype(jnp.bfloat16)
         acc[c] += lax.dot_general(scaled, weights[source], nt, preferred_element_type=jnp.float32)
 
-    for c in range(chunks):
+    def start_own(c):
         shift_copy(c).wait_recv()
         ring_copy(0, 1, c).start()
         ring_copy(1, 1, c).start()
@@ -449,6 +453,9 @@
         @pl.when(inner)
         def _():
             short_copy(0, c).start()
+
+    for c in range(AHEAD):
+        start_own(c)
     for j in range(n):
         for part in range(3):
             weight_copy(j, part).wait()
@@ -461,173 +468,190 @@
         def _(k):
             wo_own_copy(k).start()
 
-    @pl.loop(0, chunks)
-    def _(c):
-        compute(me, c)
-
-    cos, sin = tables[0], tables[1]
     lane = lax.broadcasted_iota(jnp.int32, (HD, kw), 1)
     source = lax.broadcasted_iota(jnp.int32, (HD, kw), 0)
     pick = (source == (me * kw + lane) // (2 * KV_HEADS) * 2 + lane % 2).astype(jnp.float32)
-    k_cos = lax.dot_general(cos, pick, nn, precision=lax.Precision.HIGHEST, preferred_element_type=jnp.float32)
-    k_sin = lax.dot_general(sin, pick, nn, precision=lax.Precision.HIGHEST, preferred_element_type=jnp.float32)
+    for t in range(2):
+        picked = lax.dot_general(
+            tables[t].reshape(length, HD), pick, nn, precision=lax.Precision.HIGHEST, preferred_element_type=jnp.float32
+        )
+        rotary[t] = picked.reshape(chunks, per, kw)
     per_head = kw // KV_HEADS
     target = lax.broadcasted_iota(jnp.int32, (kw, kw), 0)
     origin_row = lax.broadcasted_iota(jnp.int32, (kw, kw), 1)
     head, within = target // per_head, target % per_head
     order = (origin_row == (within // 2 * KV_HEADS + head) * 2 + within % 2).astype(jnp.bfloat16)
 
-    @pl.loop(0, hops * chunks)
-    def _(i):
-        hop = i // chunks + 1
-        turn = lax.rem(i, chunks)
-        last = hop == hops
-        c = jnp.where(last, turn // 2 + lax.rem(turn, 2) * (chunks // 2), turn)
-        low = c < chunks // 2
-        for way in range(2):
-            mine = low_or_high(way, c)
-
-            @pl.when(jnp.logical_or(jnp.logical_not(last), mine))
-            def _():
-                ring_copy(way, hop, c).wait_recv()
-
-            @pl.when(jnp.logical_and(hop < hops, sends(way, hop + 1, c)))
-            def _():
-                ring_copy(way, hop + 1, c).start()
-
-            @pl.when(jnp.logical_and(jnp.logical_and(inner, out_way == way), jnp.logical_and(hop == 1, mine)))
-            def _():
-                short_copy(1, c).start()
-
-        @pl.when(jnp.logical_and(inner, hop == hops - 2))
-        def _():
-            wo_copy(1, turn).start()
-
-        early = i - (hops - 3) * chunks
-
-        @pl.when(jnp.logical_and(corner, jnp.logical_and(early >= 0, early < EARLY)))
-        def _():
-            wo_copy(lax.rem(early, 2), early // 2).start()
-
-        @pl.loop(0, 2)
-        def _(way):
-            mine = low == (way == 0)
-
-            @pl.when(jnp.logical_or(jnp.logical_not(last), mine))
-            def _():
-                compute(ring_member(jnp.where(way == 0, position - hop, position + hop), n), c)
-
-    inverse = lax.rsqrt(
-        jnp.sum(squares[...].reshape(length, 128), axis=1, keepdims=True) * (1.0 / (n * width)) + NORM_EPS
-    )
-    k = acc[:, :, qw : qw + kw].reshape(length, kw) * inverse
-    k_rot = (k * k_cos + swap_pairs(k) * k_sin).astype(jnp.bfloat16)
-
-    def kv_copy(part, step):
+    def kv_copy(c, step):
         other = lax.rem(me + step, n)
         return pltpu.make_async_remote_copy(
-            src_ref=sent.at[other * heads // group_size, part], dst_ref=got.at[me, part],
-            send_sem=kv_send.at[part, step - 1], recv_sem=kv_recv.at[part, step - 1],
+            src_ref=sent.at[c, other * heads // group_size], dst_ref=got.at[c, me],
+            send_sem=kv_send.at[c, step - 1], recv_sem=kv_recv.at[c, step - 1],
             device_id={"mp": other}, device_id_type=MESH,
         )
 
-    def order_and_send(part, channels):
-        ordered = lax.dot_general(order, channels, nt, preferred_element_type=jnp.float32)
-        for h in range(KV_HEADS):
-            sent[h, part] = ordered[h * per_head : (h + 1) * per_head].astype(jnp.bfloat16)
+    def project(c):
+        inverse = lax.rsqrt(jnp.sum(squares[c], axis=1, keepdims=True) * (1.0 / (n * width)) + NORM_EPS)
+        k = acc[c, :, qw : qw + kw] * inverse
+        k_rot = (k * rotary[0, c] + swap_pairs(k) * rotary[1, c]).astype(jnp.bfloat16)
+        v = (acc[c, :, qw + kw :] * inverse).astype(jnp.bfloat16)
+        for part, channels in enumerate((k_rot, v)):
+            ordered = lax.dot_general(order, channels, nt, preferred_element_type=jnp.float32)
+            for h in range(KV_HEADS):
+                sent[c, h, part] = ordered[h * per_head : (h + 1) * per_head].astype(jnp.bfloat16)
         for step in range(1, n):
-            kv_copy(part, step).start()
-
-    order_and_send(0, k_rot)
-    order_and_send(1, (acc[:, :, qw + kw :].reshape(length, vw) * inverse).astype(jnp.bfloat16))
-    got[me] = sent[me * heads // group_size]
-    for h in range(heads):
-        q = acc[:, :, h * HD : (h + 1) * HD].reshape(length, HD) * inverse
-        q_ref[:, :, h * HD : (h + 1) * HD] = (
-            (q * cos + swap_pairs(q) * sin).reshape(n, rows, HD).astype(jnp.bfloat16)
-        )
-
-    def receive(part, whole):
+            kv_copy(c, step).start()
+        got[c, me] = sent[c, me * heads // group_size]
+        for h in range(heads):
+            q = acc[c, :, h * HD : (h + 1) * HD] * inverse
+            q_ref[c, :, h * HD : (h + 1) * HD] = (q * tables[0, c] + swap_pairs(q) * tables[1, c]).astype(jnp.bfloat16)
+
+    scale = 1.0 / math.sqrt(HD)
+
+    def attend(c):
         for step in range(1, n):
-            kv_copy(part, step).wait_recv()
+            kv_copy(c, step).wait_recv()
         for j in range(n):
-            heads_kv[part, j * per_head : (j + 1) * per_head] = got[j, part].astype(jnp.float32)
-        whole[...] = heads_kv[part].astype(jnp.bfloat16)
-
-    receive(0, key_head)
-    receive(1, value_head)
-
-    scale = 1.0 / math.sqrt(HD)
-
-    def attend(block):
-        row = lax.broadcasted_iota(jnp.int32, (rows, length), 0) + block * rows
-        column = lax.broadcasted_iota(jnp.int32, (rows, length), 1)
+            key_head[j * per_head : (j + 1) * per_head, part_of(c)] = got[c, j, 0]
+            value_head[j * per_head : (j + 1) * per_head, part_of(c)] = got[c, j, 1]
+        row = lax.broadcasted_iota(jnp.int32, (per, length), 0) + c * per
+        column = lax.broadcasted_iota(jnp.int32, (per, length), 1)
         for h in range(heads):
-            q = q_ref[block, :, h * HD : (h + 1) * HD]
+            q = q_ref[c, :, h * HD : (h + 1) * HD]
             scores = lax.dot_general(q, key_head[...], nn, preferred_element_type=jnp.float32) * scale
             scores = jnp.where(row >= column, scores, -1e30)
             exponent = jnp.exp(scores - jnp.max(scores, axis=1, keepdims=True))
             probs = (exponent / jnp.sum(exponent, axis=1, keepdims=True)).astype(jnp.bfloat16)
-            context[slot, block, :, h * HD : (h + 1) * HD] = lax.dot_general(
+            context[slot, part_of(c), h * HD : (h + 1) * HD] = lax.dot_general(
                 probs, value_head[...], nt, preferred_element_type=jnp.float32
             ).astype(jnp.bfloat16)
 
-    def context_copy(target, block):
-        return pltpu.make_async_remote_copy(
-            src_ref=context.at[slot, block], dst_ref=context.at[slot, block],
-            send_sem=context_send.at[target, block], recv_sem=context_recv.at[slot, block],
+        @pl.when(corner)
+        def _():
+            context_copy(0, c).start()
+
+        context_copy(1, c).start()
+
+    def context_copy(target, c):
+        return pltpu.make_async_remote_copy(
+            src_ref=context.at[slot, part_of(c)], dst_ref=context.at[slot, part_of(c)],
+            send_sem=context_send.at[target, c], recv_sem=context_recv.at[slot, c],
             device_id={"mp": 2 * inner_row + (x if target == 0 else 1 - x)}, device_id_type=MESH,
         )
 
-    def context_arrived(s, block):
-        return pltpu.make_async_remote_copy(
-            src_ref=context.at[s, block], dst_ref=context.at[s, block],
-            send_sem=context_send.at[0, block], recv_sem=context_recv.at[s, block],
+    def context_arrived(s, c):
+        return pltpu.make_async_remote_copy(
+            src_ref=context.at[s, part_of(c)], dst_ref=context.at[s, part_of(c)],
+            send_sem=context_send.at[0, c], recv_sem=context_recv.at[s, c],
             device_id={"mp": partner}, device_id_type=MESH,
         )
 
-    @pl.loop(0, n)
-    def _(i):
-        block = lax.rem(per_half - half_first + i, n)
-        attend(block)
-
-        @pl.when(corner)
-        def _():
-            context_copy(0, block).start()
-
-        context_copy(1, block).start()
-
-        @pl.when(jnp.logical_and(corner, i >= per_half - 1))
-        def _():
-            first = EARLY + (i - (per_half - 1)) * LATE
-
-            @pl.loop(first, jnp.minimum(first + LATE, 2 * pieces))
-            def _(late):
-                wo_copy(lax.rem(late, 2), late // 2).start()
+    early_pieces = chunks + chunks // 2
+
+    def wo_range(first, last):
+        @pl.loop(first, last)
+        def _(i):
+            wo_copy(lax.rem(i, 2), i // 2).start()
+
+    @pl.loop(0, chunks + hops - 1)
+    def _(wave):
+        @pl.when(wave + AHEAD < chunks)
+        def _():
+            start_own(wave + AHEAD)
+
+        @pl.when(wave < chunks)
+        def _():
+            compute(me, wave)
+
+        @pl.loop(1, hops + 1)
+        def _(hop):
+            c = wave - (hop - 1)
+            last = hop == hops
+
+            @pl.when(jnp.logical_and(c >= 0, c < chunks))
+            def _():
+                for way in range(2):
+                    mine = own_parity(way, c)
+
+                    @pl.when(jnp.logical_or(jnp.logical_not(last), mine))
+                    def _():
+                        ring_copy(way, hop, c).wait_recv()
+
+                    @pl.when(jnp.logical_and(hop < hops, sends(way, hop + 1, c)))
+                    def _():
+                        ring_copy(way, hop + 1, c).start()
+
+                    @pl.when(jnp.logical_and(jnp.logical_and(inner, out_way == way), jnp.logical_and(hop == 1, mine)))
+                    def _():
+                        short_copy(1, c).start()
+
+                @pl.when(jnp.logical_and(inner, hop == hops - 2))
+                def _():
+                    @pl.loop(c * pieces // chunks, (c + 1) * pieces // chunks)
+                    def _(k):
+                        wo_copy(1, k).start()
+
+                @pl.when(jnp.logical_and(corner, hop == hops - 2))
+                def _():
+                    first = c + c // 2
+                    wo_range(first, first + 1 + lax.rem(c, 2))
+
+                @pl.loop(0, 2)
+                def _(way):
+                    @pl.when(jnp.logical_or(jnp.logical_not(last), own_parity(way, c)))
+                    def _():
+                        compute(ring_member(jnp.where(way == 0, position - hop, position + hop), n), c)
+
+        @pl.when(wave >= hops - 1)
+        def _():
+            project(wave - (hops - 1))
+
+        @pl.when(wave >= hops - 1 + LAG)
+        def _():
+            attend(wave - (hops - 1) - LAG)
+
+    @pl.loop(chunks - LAG, chunks)
+    def _(c):
+        attend(c)
+
+    @pl.when(corner)
+    def _():
+        wo_range(early_pieces, 2 * pieces)
 
     slots = context.shape[0]
-
-    def term(first, k):
-        total = jnp.zeros((per_half * rows, piece_width), jnp.float32)
+    parts = 2
+    blocks = per_half // parts
+    half_chunks = chunks // 2
+    turns = parts * pieces
+
+    def turn_of(i):
+        first = i < turns // 2
+        late = i - turns // 2
+        part = jnp.where(first, i // (pieces // 2), lax.rem(late, parts))
+        piece = jnp.where(first, lax.rem(i, pieces // 2), pieces // 2 + late // parts)
+        return part, piece
+
+    def term(group, part, k):
+        start = pl.multiple_of((group * per_half + part * blocks) * rows, blocks * rows)
+        total = jnp.zeros((blocks * rows, piece_width), jnp.float32)
         for s in range(slots):
             total += jnp.dot(
-                context[s, pl.ds(first, per_half)].reshape(per_half * rows, qw), w_half[k, s],
-                preferred_element_type=jnp.float32,
+                context[s, pl.ds(start, blocks * rows)], w_half[k, s], preferred_element_type=jnp.float32
             )
         return total
 
-    def mid_copy(k):
-        return pltpu.make_async_remote_copy(
-            src_ref=leaving.at[k], dst_ref=entering.at[k],
-            send_sem=mid_send.at[k], recv_sem=mid_recv.at[k],
+    def mid_copy(i):
+        return pltpu.make_async_remote_copy(
+            src_ref=leaving.at[i], dst_ref=entering.at[i],
+            send_sem=mid_send.at[i], recv_sem=mid_recv.at[i],
             device_id={"mp": opposite}, device_id_type=MESH,
         )
 
-    def final_copy(k, b):
-        return pltpu.make_async_remote_copy(
-            src_ref=summed.at[k, b], dst_ref=final.at[x, k],
-            send_sem=final_send.at[k, b], recv_sem=final_recv.at[x, k],
-            device_id={"mp": half_first + b}, device_id_type=MESH,
+    def final_copy(i, part, k, b):
+        return pltpu.make_async_remote_copy(
+            src_ref=summed.at[i, b], dst_ref=final.at[x, k],
+            send_sem=final_send.at[i, b], recv_sem=final_recv.at[x, k],
+            device_id={"mp": half_first + part * blocks + b}, device_id_type=MESH,
         )
 
     def final_arrived(side, k):
@@ -637,46 +661,53 @@
             device_id={"mp": partner}, device_id_type=MESH,
         )
 
-    def contexts_arrived(first):
-        for s in range(slots):
-            @pl.when(slot != s)
-            def _():
-                @pl.loop(0, per_half)
-                def _(b):
-                    context_arrived(s, first + b).wait_recv()
+    def contexts_arrived(group, i):
+        @pl.when(jnp.logical_or(i == 0, i == pieces // 2))
+        def _():
+            first = group * half_chunks + jnp.where(i == 0, 0, half_chunks - 1)
+            for s in range(slots):
+                @pl.when(slot != s)
+                def _():
+                    @pl.loop(first, jnp.where(i == 0, first + half_chunks - 1, first + 1))
+                    def _(c):
+                        context_arrived(s, c).wait_recv()
 
     @pl.when(inner)
     def _():
-        contexts_arrived(per_half - half_first)
-
-        @pl.loop(0, pieces + LEAD)
+        @pl.loop(0, turns + LEAD)
         def _(i):
-            @pl.when(i < pieces)
+            @pl.when(i < turns)
             def _():
-                wo_own_copy(i).wait()
-                for s in range(slots):
-                    @pl.when(slot != s)
-                    def _():
-                        wo_arrived(s, i).wait_recv()
-                leaving[i] = term(per_half - half_first, i).astype(jnp.bfloat16)
+                part, k = turn_of(i)
+
+                @pl.when(jnp.where(i < turns // 2, i < pieces // 2, part == 0))
+                def _():
+                    wo_own_copy(k).wait()
+                    for s in range(slots):
+                        @pl.when(slot != s)
+                        def _():
+                            wo_arrived(s, k).wait_recv()
+                contexts_arrived(1 - half, i)
+                leaving[i] = term(1 - half, part, k).astype(jnp.bfloat16)
                 mid_copy(i).start()
-
-            @pl.when(i == LEAD)
-            def _():
-                contexts_arrived(half_first)
 
             @pl.when(i >= LEAD)
             def _():
-                k = i - LEAD
-                value = term(half_first, k)
-                mid_copy(k).wait_recv()
-                value = value + entering[k].astype(jnp.float32)
-                summed[k] = value.astype(jnp.bfloat16).reshape(per_half, rows, piece_width)
-                for b in range(per_half):
-                    @pl.when(half_first + b != me)
+                j = i - LEAD
+                part, k = turn_of(j)
+                contexts_arrived(half, j)
+                value = term(half, part, k)
+                mid_copy(j).wait_recv()
+                value = value + entering[j].astype(jnp.float32)
+                summed[j] = value.astype(jnp.bfloat16).reshape(blocks, rows, piece_width)
+                for b in range(blocks):
+                    @pl.when(half_first + part * blocks + b != me)
                     def _():
-                        final_copy(k, b).start()
-                final[x, k] = summed[k, me - half_first]
+                        final_copy(j, part, k, b).start()
+
+                    @pl.when(half_first + part * blocks + b == me)
+                    def _():
+                        final[x, k] = summed[j, b]
 
     @pl.loop(0, pieces)
     def _(k):
@@ -690,14 +721,21 @@
             value = final[side, k]
             attended_ref[:, columns] = value
             stream_ref[:, columns] = (
-                x_all[start // width, me, :, within_block].astype(jnp.float32) + value.astype(jnp.float32)
+                x_all[start // width, pl.ds(pl.multiple_of(me * rows, rows), rows), within_block].astype(jnp.float32) + value.astype(jnp.float32)
             ).astype(jnp.bfloat16)
 
     for c in range(chunks):
         shift_copy(c).wait_send()
-    for part in range(2):
+
+    @pl.loop(0, chunks)
+    def _(c):
         for step in range(1, n):
-            kv_copy(part, step).wait_send()
+            kv_copy(c, step).wait_send()
+
+        @pl.when(corner)
+        def _():
+            context_copy(0, c).wait_send()
+        context_copy(1, c).wait_send()
 
     @pl.loop(0, hops * chunks)
     def _(i):
@@ -708,13 +746,6 @@
             def _():
                 ring_copy(way, hop, c).wait_send()
 
-    @pl.loop(0, n)
-    def _(block):
-        @pl.when(corner)
-        def _():
-            context_copy(0, block).wait_send()
-        context_copy(1, block).wait_send()
-
     @pl.loop(0, pieces)
     def _(k):
         wo_copy(1, k).wait_send()
@@ -723,20 +754,23 @@
         def _():
             wo_copy(0, k).wait_send()
 
-        @pl.when(inner)
-        def _():
-            mid_copy(k).wait_send()
-            for b in range(per_half):
-                @pl.when(half_first + b != me)
+    @pl.when(inner)
+    def _():
+        @pl.loop(0, turns)
+        def _(i):
+            part, k = turn_of(i)
+            mid_copy(i).wait_send()
+            for b in range(blocks):
+                @pl.when(half_first + part * blocks + b != me)
                 def _():
-                    final_copy(k, b).wait_send()
+                    final_copy(i, part, k, b).wait_send()
 
     @pl.when(inner)
     def _():
         for c in range(chunks):
             short_copy(0, c).wait_send()
 
-            @pl.when((c < chunks // 2) == (out_way == 0))
+            @pl.when(own_parity(out_way, c))
             def _():
                 short_copy(1, c).wait_send()
 
@@ -762,36 +796,38 @@
     hbm = pl.BlockSpec(memory_space=pltpu.HBM)
     bf16, f32 = jnp.bfloat16, jnp.float32
     dma = pltpu.SemaphoreType.DMA
-    operands = (
-        arriving[0].reshape(n, rows, width),
-        norm_gain[0].reshape(n, 1, width),
-        w_query[0], w_key[0], w_value[0], w_out[0], jnp.asarray(tables),
-    )
-    shared = [
-        pltpu.VMEM((n, rows, width), bf16),
-        pltpu.VMEM((n, 1, width), bf16),
-        pltpu.VMEM((2, length, HD), f32),
-        pltpu.VMEM((n, n, rows, width), bf16),
-        pltpu.VMEM((n, qw + kw + vw, width), bf16),
-        pltpu.VMEM((chunks, length // chunks, qw + kw + vw), f32),
-        pltpu.VMEM((chunks, length // chunks, 128), f32),
-        pltpu.VMEM((KV_HEADS, 2, kw // KV_HEADS, length), bf16),
-        pltpu.VMEM((n, 2, kw // KV_HEADS, length), bf16),
-        pltpu.VMEM((2, HD, length), f32),
-        pltpu.VMEM((HD, length), bf16),
-        pltpu.VMEM((HD, length), bf16),
-        pltpu.VMEM((n, rows, qw), bf16),
-    ]
     if n == 8:
         pieces = 8
         piece_width = full // (2 * pieces)
+        per = 128
+        chunks = length // per
+        per_head = kw // KV_HEADS
+        blocks = n // 4
         kernel = grid_kernel
-        scratch = shared + [
-            pltpu.VMEM((4, n, rows, qw), bf16),
+        operands = (
+            arriving[0],
+            norm_gain[0].reshape(n, 1, width),
+            w_query[0], w_key[0], w_value[0], w_out[0], jnp.asarray(tables.reshape(2, chunks, per, HD)),
+        )
+        scratch = [
+            pltpu.VMEM((length, width), bf16),
+            pltpu.VMEM((n, 1, width), bf16),
+            pltpu.VMEM((2, chunks, per, HD), f32),
+            pltpu.VMEM((n, length, width), bf16),
+            pltpu.VMEM((n, qw + kw + vw, width), bf16),
+            pltpu.VMEM((chunks, per, qw + kw + vw), f32),
+            pltpu.VMEM((chunks, per, 128), f32),
+            pltpu.VMEM((2, chunks, per, kw), f32),
+            pltpu.VMEM((chunks, KV_HEADS, 2, per_head, per), bf16),
+            pltpu.VMEM((chunks, n, 2, per_head, per), bf16),
+            pltpu.VMEM((HD, length), bf16),
+            pltpu.VMEM((HD, length), bf16),
+            pltpu.VMEM((chunks, per, qw), bf16),
+            pltpu.VMEM((4, length, qw), bf16),
             pltpu.VMEM((pieces, 4, qw, piece_width), bf16),
-            pltpu.VMEM((pieces, length // 2, piece_width), bf16),
-            pltpu.VMEM((pieces, length // 2, piece_width), bf16),
-            pltpu.VMEM((pieces, n // 2, rows, piece_width), bf16),
+            pltpu.VMEM((2 * pieces, blocks * rows, piece_width), bf16),
+            pltpu.VMEM((2 * pieces, blocks * rows, piece_width), bf16),
+            pltpu.VMEM((2 * pieces, blocks, rows, piece_width), bf16),
             pltpu.VMEM((2, pieces, rows, piece_width), bf16),
             dma(()),
             dma(()),
@@ -802,21 +838,39 @@
             dma((2, n // 2, chunks)),
             dma((2, n // 2, chunks)),
             dma((2, chunks)),
-            dma((2, n - 1)),
-            dma((2, n - 1)),
+            dma((chunks, n - 1)),
+            dma((chunks, n - 1)),
             dma((pieces,)),
             dma((2, pieces)),
             dma((4, pieces)),
-            dma((2, n)),
-            dma((4, n)),
-            dma((pieces,)),
-            dma((pieces,)),
-            dma((pieces, n // 2)),
+            dma((2, chunks)),
+            dma((4, chunks)),
+            dma((2 * pieces,)),
+            dma((2 * pieces,)),
+            dma((2 * pieces, blocks)),
             dma((2, pieces)),
         ]
     else:
         kernel = ring_kernel
-        scratch = shared + [
+        operands = (
+            arriving[0].reshape(n, rows, width),
+            norm_gain[0].reshape(n, 1, width),
+            w_query[0], w_key[0], w_value[0], w_out[0], jnp.asarray(tables),
+        )
+        scratch = [
+            pltpu.VMEM((n, rows, width), bf16),
+            pltpu.VMEM((n, 1, width), bf16),
+            pltpu.VMEM((2, length, HD), f32),
+            pltpu.VMEM((n, n, rows, width), bf16),
+            pltpu.VMEM((n, qw + kw + vw, width), bf16),
+            pltpu.VMEM((chunks, length // chunks, qw + kw + vw), f32),
+            pltpu.VMEM((chunks, length // chunks, 128), f32),
+            pltpu.VMEM((KV_HEADS, 2, kw // KV_HEADS, length), bf16),
+            pltpu.VMEM((n, 2, kw // KV_HEADS, length), bf16),
+            pltpu.VMEM((2, HD, length), f32),
+            pltpu.VMEM((HD, length), bf16),
+            pltpu.VMEM((HD, length), bf16),
+            pltpu.VMEM((n, rows, qw), bf16),
             pltpu.VMEM((qw, full), bf16),
             pltpu.VMEM((n, rows, qw), bf16),
             pltpu.VMEM((2, n, pieces, rows, full // (2 * pieces)), bf16),

time: 235 us -> 224 us (0.953)
  the two profiles are of different devices: /device:TPU:4 before, /device:TPU:30 now
where the time goes in v2:
time: 224 us
  Pallas kernels  221 us (99%)
  local copies, waits for them, and re-layouts  2.29 us (1%)
    pallas_call x1, Pallas kernels, local(): pl.pallas_call(functools.partial(kernel, n, chunks, pieces), name='layer'...  221 us

profile of v2, /device:TPU:30, one launch (start us, length us, event | category | flops | bytes accessed | tf_op | source)
XLA Modules:
  0.0 223.5 jit_solution(12315138204454140455)
XLA Ops:
  0.6 220.6 %layer.1 = (bf16[96,8192]{1,0:T(8,128)(2,1)S(1)}, bf16[96,8192]{1,0:T(8,128)(2,1)S(1)}) custom-call(bf16[768,1024]{1,0:T(8,128)(2,1)} %bitcast.14, bf16[8,1,1024]{2,1,0:T(2,128)(2,1)} %bitcast.15, bf16[256,8192]{1,0:T(8,128)(2,1)} %bitcast.10, bf16[128,8192]{1,0:T(8,128)(2,1)} %bitcast.12, bf16[128,8192]{1,0:T(8,128)(2,1)} %bitcast.13, ...), custom_call_target="tpu_custom_call" | custom-call | tf_op jit(solution)/shard_map/layer/pallas_call | solution.py:891
  221.2 1.1 copy.11
  222.4 1.1 copy.12

commit v3 on v2

--- a/solution.py
+++ b/solution.py
@@ -16,8 +16,10 @@
 MESH = pl.DeviceIdType.MESH
 VMEM_LIMIT = 63500000
 AHEAD = 2
-LAG = 2
-LEAD = 3
+LEAD = 4
+LAST = 2
+EARLY_CORNER = 8
+EARLY_INNER = 4
 
 
 def ring_position(member, n):
@@ -372,30 +374,29 @@
             device_id={"section": following}, device_id_type=MESH,
         )
 
-    def ring_copy(way, hop, c):
+    def share_of(way, c):
+        return pl.ds(pl.multiple_of(c * per + way * (per // 2), per // 2), per // 2)
+
+    def ring_copy(way, hop, c, shared):
         origin = ring_member(position - (hop - 1) if way == 0 else position + (hop - 1), n)
-        return pltpu.make_async_remote_copy(
-            src_ref=x_all.at[origin, part_of(c)],
-            dst_ref=x_all.at[origin, part_of(c)],
+        tokens = share_of(way, c) if shared else part_of(c)
+        return pltpu.make_async_remote_copy(
+            src_ref=x_all.at[origin, tokens], dst_ref=x_all.at[origin, tokens],
             send_sem=ring_send.at[way, hop - 1, c], recv_sem=ring_recv.at[way, hop - 1, c],
             device_id={"mp": right if way == 0 else left}, device_id_type=MESH,
         )
 
     def short_copy(late, c):
         origin = beyond if late else me
-        return pltpu.make_async_remote_copy(
-            src_ref=x_all.at[origin, part_of(c)],
-            dst_ref=x_all.at[origin, part_of(c)],
+        tokens = share_of(out_way, c) if late else part_of(c)
+        return pltpu.make_async_remote_copy(
+            src_ref=x_all.at[origin, tokens], dst_ref=x_all.at[origin, tokens],
             send_sem=short_send.at[late, c], recv_sem=ring_recv.at[out_way, hops - 2 + late, c],
             device_id={"mp": partner}, device_id_type=MESH,
         )
 
-    def own_parity(way, c):
-        return lax.rem(c, 2) == way
-
-    def sends(way, hop, c):
-        on = jnp.logical_not(jnp.logical_and(jnp.logical_and(corner, out_way == way), hop >= hops - 1))
-        return jnp.logical_and(on, jnp.logical_or(hop < hops, own_parity(way, c)))
+    def through(way):
+        return jnp.logical_or(inner, out_way != way)
 
     piece_width = w_half.shape[3]
 
@@ -447,8 +448,8 @@
 
     def start_own(c):
         shift_copy(c).wait_recv()
-        ring_copy(0, 1, c).start()
-        ring_copy(1, 1, c).start()
+        ring_copy(0, 1, c, False).start()
+        ring_copy(1, 1, c, False).start()
 
         @pl.when(inner)
         def _():
@@ -506,7 +507,7 @@
             q = acc[c, :, h * HD : (h + 1) * HD] * inverse
             q_ref[c, :, h * HD : (h + 1) * HD] = (q * tables[0, c] + swap_pairs(q) * tables[1, c]).astype(jnp.bfloat16)
 
-    scale = 1.0 / math.sqrt(HD)
+    scale = 1.0 / (math.sqrt(HD) * math.log(2.0))
 
     def attend(c):
         for step in range(1, n):
@@ -518,10 +519,10 @@
         column = lax.broadcasted_iota(jnp.int32, (per, length), 1)
         for h in range(heads):
             q = q_ref[c, :, h * HD : (h + 1) * HD]
-            scores = lax.dot_general(q, key_head[...], nn, preferred_element_type=jnp.float32) * scale
+            scores = lax.dot_general(q, key_head[...], nn, preferred_element_type=jnp.float32)
             scores = jnp.where(row >= column, scores, -1e30)
-            exponent = jnp.exp(scores - jnp.max(scores, axis=1, keepdims=True))
-            probs = (exponent / jnp.sum(exponent, axis=1, keepdims=True)).astype(jnp.bfloat16)
+            exponent = jnp.exp2((scores - jnp.max(scores, axis=1, keepdims=True)) * scale)
+            probs = (exponent * (1.0 / jnp.sum(exponent, axis=1, keepdims=True))).astype(jnp.bfloat16)
             context[slot, part_of(c), h * HD : (h + 1) * HD] = lax.dot_general(
                 probs, value_head[...], nt, preferred_element_type=jnp.float32
             ).astype(jnp.bfloat16)
@@ -545,8 +546,6 @@
             send_sem=context_send.at[0, c], recv_sem=context_recv.at[s, c],
             device_id={"mp": partner}, device_id_type=MESH,
         )
-
-    early_pieces = chunks + chunks // 2
 
     def wo_range(first, last):
         @pl.loop(first, last)
@@ -563,6 +562,10 @@
         def _():
             compute(me, wave)
 
+        @pl.when(jnp.logical_and(wave > hops, wave < chunks + hops - 2))
+        def _():
+            attend(wave - hops - 1)
+
         @pl.loop(1, hops + 1)
         def _(hop):
             c = wave - (hop - 1)
@@ -571,56 +574,50 @@
             @pl.when(jnp.logical_and(c >= 0, c < chunks))
             def _():
                 for way in range(2):
-                    mine = own_parity(way, c)
-
-                    @pl.when(jnp.logical_or(jnp.logical_not(last), mine))
+                    @pl.when(jnp.logical_not(last))
                     def _():
-                        ring_copy(way, hop, c).wait_recv()
-
-                    @pl.when(jnp.logical_and(hop < hops, sends(way, hop + 1, c)))
+                        ring_copy(way, hop, c, False).wait_recv()
+
+                    @pl.when(last)
                     def _():
-                        ring_copy(way, hop + 1, c).start()
-
-                    @pl.when(jnp.logical_and(jnp.logical_and(inner, out_way == way), jnp.logical_and(hop == 1, mine)))
+                        ring_copy(way, hop, c, True).wait_recv()
+
+                    @pl.when(jnp.logical_or(hop < hops - 2, jnp.logical_and(hop == hops - 2, through(way))))
+                    def _():
+                        ring_copy(way, hop + 1, c, False).start()
+
+                    @pl.when(jnp.logical_and(hop == hops - 1, through(way)))
+                    def _():
+                        ring_copy(way, hop + 1, c, True).start()
+
+                    @pl.when(jnp.logical_and(jnp.logical_and(inner, out_way == way), hop == 1))
                     def _():
                         short_copy(1, c).start()
 
                 @pl.when(jnp.logical_and(inner, hop == hops - 2))
                 def _():
-                    @pl.loop(c * pieces // chunks, (c + 1) * pieces // chunks)
+                    @pl.loop(c * EARLY_INNER // chunks, (c + 1) * EARLY_INNER // chunks)
                     def _(k):
                         wo_copy(1, k).start()
 
                 @pl.when(jnp.logical_and(corner, hop == hops - 2))
                 def _():
-                    first = c + c // 2
-                    wo_range(first, first + 1 + lax.rem(c, 2))
-
-                @pl.loop(0, 2)
+                    wo_range(c * EARLY_CORNER // chunks, (c + 1) * EARLY_CORNER // chunks)
+
+                @pl.loop(0, jnp.where(last, 1, 2))
                 def _(way):
-                    @pl.when(jnp.logical_or(jnp.logical_not(last), own_parity(way, c)))
-                    def _():
-                        compute(ring_member(jnp.where(way == 0, position - hop, position + hop), n), c)
+                    compute(ring_member(jnp.where(way == 0, position - hop, position + hop), n), c)
+
+                @pl.when(jnp.logical_and(c == chunks - 1, hop == hops - 1))
+                def _():
+                    attend(chunks - 3)
 
         @pl.when(wave >= hops - 1)
         def _():
             project(wave - (hops - 1))
 
-        @pl.when(wave >= hops - 1 + LAG)
-        def _():
-            attend(wave - (hops - 1) - LAG)
-
-    @pl.loop(chunks - LAG, chunks)
-    def _(c):
-        attend(c)
-
-    @pl.when(corner)
-    def _():
-        wo_range(early_pieces, 2 * pieces)
-
     slots = context.shape[0]
-    parts = 2
-    blocks = per_half // parts
+    parts = per_half
     half_chunks = chunks // 2
     turns = parts * pieces
 
@@ -632,11 +629,11 @@
         return part, piece
 
     def term(group, part, k):
-        start = pl.multiple_of((group * per_half + part * blocks) * rows, blocks * rows)
-        total = jnp.zeros((blocks * rows, piece_width), jnp.float32)
+        start = pl.multiple_of((group * per_half + part) * rows, rows)
+        total = jnp.zeros((rows, piece_width), jnp.float32)
         for s in range(slots):
             total += jnp.dot(
-                context[s, pl.ds(start, blocks * rows)], w_half[k, s], preferred_element_type=jnp.float32
+                context[s, pl.ds(start, rows)], w_half[k, s], preferred_element_type=jnp.float32
             )
         return total
 
@@ -647,35 +644,49 @@
             device_id={"mp": opposite}, device_id_type=MESH,
         )
 
-    def final_copy(i, part, k, b):
-        return pltpu.make_async_remote_copy(
-            src_ref=summed.at[i, b], dst_ref=final.at[x, k],
-            send_sem=final_send.at[i, b], recv_sem=final_recv.at[x, k],
-            device_id={"mp": half_first + part * blocks + b}, device_id_type=MESH,
+    def final_copy(i):
+        part, k = turn_of(i)
+        return pltpu.make_async_remote_copy(
+            src_ref=summed.at[i], dst_ref=final.at[x, k],
+            send_sem=final_send.at[i], recv_sem=final_recv.at[x, k],
+            device_id={"mp": half_first + part}, device_id_type=MESH,
         )
 
     def final_arrived(side, k):
         return pltpu.make_async_remote_copy(
             src_ref=final.at[side, k], dst_ref=final.at[side, k],
-            send_sem=final_send.at[k, 0], recv_sem=final_recv.at[side, k],
+            send_sem=final_send.at[k], recv_sem=final_recv.at[side, k],
             device_id={"mp": partner}, device_id_type=MESH,
         )
 
     def contexts_arrived(group, i):
-        @pl.when(jnp.logical_or(i == 0, i == pieces // 2))
-        def _():
-            first = group * half_chunks + jnp.where(i == 0, 0, half_chunks - 1)
+        step = pieces // 2
+
+        @pl.when(jnp.logical_and(lax.rem(i, step) == 0, i // step < half_chunks))
+        def _():
             for s in range(slots):
                 @pl.when(slot != s)
                 def _():
-                    @pl.loop(first, jnp.where(i == 0, first + half_chunks - 1, first + 1))
-                    def _(c):
-                        context_arrived(s, c).wait_recv()
-
-    @pl.when(inner)
-    def _():
-        @pl.loop(0, turns + LEAD)
-        def _(i):
+                    context_arrived(s, group * half_chunks + i // step).wait_recv()
+
+    @pl.loop(0, turns + LEAD)
+    def _(i):
+        @pl.when(jnp.logical_or(i == LAST - 1, i == LAST))
+        def _():
+            attend(chunks - 2 + i - (LAST - 1))
+
+        @pl.when(jnp.logical_and(corner, i == LAST))
+        def _():
+            wo_range(EARLY_CORNER, 2 * pieces)
+
+        @pl.when(inner)
+        def _():
+            @pl.when(i == LAST)
+            def _():
+                @pl.loop(EARLY_INNER, pieces)
+                def _(k):
+                    wo_copy(1, k).start()
+
             @pl.when(i < turns)
             def _():
                 part, k = turn_of(i)
@@ -699,15 +710,16 @@
                 value = term(half, part, k)
                 mid_copy(j).wait_recv()
                 value = value + entering[j].astype(jnp.float32)
-                summed[j] = value.astype(jnp.bfloat16).reshape(blocks, rows, piece_width)
-                for b in range(blocks):
-                    @pl.when(half_first + part * blocks + b != me)
-                    def _():
-                        final_copy(j, part, k, b).start()
-
-                    @pl.when(half_first + part * blocks + b == me)
-                    def _():
-                        final[x, k] = summed[j, b]
+                value = value.astype(jnp.bfloat16)
+
+                @pl.when(half_first + part != me)
+                def _():
+                    summed[j] = value
+                    final_copy(j).start()
+
+                @pl.when(half_first + part == me)
+                def _():
+                    final[x, k] = value
 
     @pl.loop(0, pieces)
     def _(k):
@@ -737,14 +749,17 @@
             context_copy(0, c).wait_send()
         context_copy(1, c).wait_send()
 
-    @pl.loop(0, hops * chunks)
-    def _(i):
-        hop = i // chunks + 1
-        c = lax.rem(i, chunks)
+    @pl.loop(0, chunks)
+    def _(c):
         for way in range(2):
-            @pl.when(sends(way, hop, c))
-            def _():
-                ring_copy(way, hop, c).wait_send()
+            @pl.loop(1, hops - 1)
+            def _(hop):
+                ring_copy(way, hop, c, False).wait_send()
+
+            @pl.when(through(way))
+            def _():
+                ring_copy(way, hops - 1, c, False).wait_send()
+                ring_copy(way, hops, c, True).wait_send()
 
     @pl.loop(0, pieces)
     def _(k):
@@ -760,19 +775,16 @@
         def _(i):
             part, k = turn_of(i)
             mid_copy(i).wait_send()
-            for b in range(blocks):
-                @pl.when(half_first + part * blocks + b != me)
-                def _():
-                    final_copy(i, part, k, b).wait_send()
+
+            @pl.when(half_first + part != me)
+            def _():
+                final_copy(i).wait_send()
 
     @pl.when(inner)
     def _():
         for c in range(chunks):
             short_copy(0, c).wait_send()
-
-            @pl.when(own_parity(out_way, c))
-            def _():
-                short_copy(1, c).wait_send()
+            short_copy(1, c).wait_send()
 
 
 def rotary_tables(length):
@@ -802,7 +814,7 @@
         per = 128
         chunks = length // per
         per_head = kw // KV_HEADS
-        blocks = n // 4
+        turns = n // 2 * pieces
         kernel = grid_kernel
         operands = (
             arriving[0],
@@ -825,9 +837,9 @@
             pltpu.VMEM((chunks, per, qw), bf16),
             pltpu.VMEM((4, length, qw), bf16),
             pltpu.VMEM((pieces, 4, qw, piece_width), bf16),
-            pltpu.VMEM((2 * pieces, blocks * rows, piece_width), bf16),
-            pltpu.VMEM((2 * pieces, blocks * rows, piece_width), bf16),
-            pltpu.VMEM((2 * pieces, blocks, rows, piece_width), bf16),
+            pltpu.VMEM((turns, rows, piece_width), bf16),
+            pltpu.VMEM((turns, rows, piece_width), bf16),
+            pltpu.VMEM((turns, rows, piece_width), bf16),
             pltpu.VMEM((2, pieces, rows, piece_width), bf16),
             dma(()),
             dma(()),
@@ -845,9 +857,9 @@
             dma((4, pieces)),
             dma((2, chunks)),
             dma((4, chunks)),
-            dma((2 * pieces,)),
-            dma((2 * pieces,)),
-            dma((2 * pieces, blocks)),
+            dma((turns,)),
+            dma((turns,)),
+            dma((turns,)),
             dma((2, pieces)),
         ]
     else:

time: 224 us -> 216 us (0.964)
  the two profiles are of different devices: /device:TPU:30 before, /device:TPU:4 now
where the time goes in v3:
time: 216 us; the launch traced here: 214 us
  Pallas kernels  211 us (98%)
  local copies, waits for them, and re-layouts  2.29 us (1%)
    pallas_call x1, Pallas kernels, local(): pl.pallas_call(functools.partial(kernel, n, chunks, pieces), name='layer'...  211 us

profile of v3, /device:TPU:4, one launch (start us, length us, event | category | flops | bytes accessed | tf_op | source)
XLA Modules:
  0.0 213.7 jit_solution(16733575277445635502)
XLA Ops:
  0.6 210.7 %layer.1 = (bf16[96,8192]{1,0:T(8,128)(2,1)S(1)}, bf16[96,8192]{1,0:T(8,128)(2,1)S(1)}) custom-call(bf16[768,1024]{1,0:T(8,128)(2,1)} %bitcast.14, bf16[8,1,1024]{2,1,0:T(2,128)(2,1)} %bitcast.15, bf16[256,8192]{1,0:T(8,128)(2,1)} %bitcast.10, bf16[128,8192]{1,0:T(8,128)(2,1)} %bitcast.12, bf16[128,8192]{1,0:T(8,128)(2,1)} %bitcast.13, ...), custom_call_target="tpu_custom_call" | custom-call | tf_op jit(solution)/shard_map/layer/pallas_call | solution.py:903
  211.4 1.1 copy.11
  212.5 1.1 copy.12

commit v4 on v3

--- a/solution.py
+++ b/solution.py
@@ -17,9 +17,15 @@
 VMEM_LIMIT = 63500000
 AHEAD = 2
 LEAD = 4
-LAST = 2
-EARLY_CORNER = 8
-EARLY_INNER = 4
+FIRST = 2
+START = 1
+LAST = 3
+SLOT_CORNER = 2
+SLOT_INNER = 2
+EARLY_CORNER = 7
+EARLY_INNER = 5
+MORE = 1
+HEAD = 3
 
 
 def ring_position(member, n):
@@ -547,85 +553,15 @@
             device_id={"mp": partner}, device_id_type=MESH,
         )
 
-    def wo_range(first, last):
-        @pl.loop(first, last)
-        def _(i):
-            wo_copy(lax.rem(i, 2), i // 2).start()
-
-    @pl.loop(0, chunks + hops - 1)
-    def _(wave):
-        @pl.when(wave + AHEAD < chunks)
-        def _():
-            start_own(wave + AHEAD)
-
-        @pl.when(wave < chunks)
-        def _():
-            compute(me, wave)
-
-        @pl.when(jnp.logical_and(wave > hops, wave < chunks + hops - 2))
-        def _():
-            attend(wave - hops - 1)
-
-        @pl.loop(1, hops + 1)
-        def _(hop):
-            c = wave - (hop - 1)
-            last = hop == hops
-
-            @pl.when(jnp.logical_and(c >= 0, c < chunks))
-            def _():
-                for way in range(2):
-                    @pl.when(jnp.logical_not(last))
-                    def _():
-                        ring_copy(way, hop, c, False).wait_recv()
-
-                    @pl.when(last)
-                    def _():
-                        ring_copy(way, hop, c, True).wait_recv()
-
-                    @pl.when(jnp.logical_or(hop < hops - 2, jnp.logical_and(hop == hops - 2, through(way))))
-                    def _():
-                        ring_copy(way, hop + 1, c, False).start()
-
-                    @pl.when(jnp.logical_and(hop == hops - 1, through(way)))
-                    def _():
-                        ring_copy(way, hop + 1, c, True).start()
-
-                    @pl.when(jnp.logical_and(jnp.logical_and(inner, out_way == way), hop == 1))
-                    def _():
-                        short_copy(1, c).start()
-
-                @pl.when(jnp.logical_and(inner, hop == hops - 2))
-                def _():
-                    @pl.loop(c * EARLY_INNER // chunks, (c + 1) * EARLY_INNER // chunks)
-                    def _(k):
-                        wo_copy(1, k).start()
-
-                @pl.when(jnp.logical_and(corner, hop == hops - 2))
-                def _():
-                    wo_range(c * EARLY_CORNER // chunks, (c + 1) * EARLY_CORNER // chunks)
-
-                @pl.loop(0, jnp.where(last, 1, 2))
-                def _(way):
-                    compute(ring_member(jnp.where(way == 0, position - hop, position + hop), n), c)
-
-                @pl.when(jnp.logical_and(c == chunks - 1, hop == hops - 1))
-                def _():
-                    attend(chunks - 3)
-
-        @pl.when(wave >= hops - 1)
-        def _():
-            project(wave - (hops - 1))
-
     slots = context.shape[0]
     parts = per_half
     half_chunks = chunks // 2
     turns = parts * pieces
 
     def turn_of(i):
-        first = i < turns // 2
-        late = i - turns // 2
-        part = jnp.where(first, i // (pieces // 2), lax.rem(late, parts))
-        piece = jnp.where(first, lax.rem(i, pieces // 2), pieces // 2 + late // parts)
+        late = i - HEAD * parts
+        part = jnp.where(late < 0, i // HEAD, lax.rem(i - HEAD * parts + turns, parts))
+        piece = jnp.where(late < 0, lax.rem(i, HEAD), HEAD + late // parts)
         return part, piece
 
     def term(group, part, k):
@@ -660,16 +596,107 @@
         )
 
     def contexts_arrived(group, i):
-        step = pieces // 2
-
-        @pl.when(jnp.logical_and(lax.rem(i, step) == 0, i // step < half_chunks))
+        @pl.when(jnp.logical_and(lax.rem(i, HEAD) == 0, i // HEAD < half_chunks))
         def _():
             for s in range(slots):
                 @pl.when(slot != s)
                 def _():
-                    context_arrived(s, group * half_chunks + i // step).wait_recv()
-
-    @pl.loop(0, turns + LEAD)
+                    context_arrived(s, group * half_chunks + i // HEAD).wait_recv()
+
+    def send_turn(i):
+        part, k = turn_of(i)
+
+        @pl.when(part == 0)
+        def _():
+            wo_own_copy(k).wait()
+            for s in range(slots):
+                @pl.when(slot != s)
+                def _():
+                    wo_arrived(s, k).wait_recv()
+        contexts_arrived(1 - half, i)
+        leaving[i] = term(1 - half, part, k).astype(jnp.bfloat16)
+        mid_copy(i).start()
+
+    def wo_range(first, last):
+        @pl.loop(first, last)
+        def _(i):
+            wo_copy(lax.rem(i, 2), i // 2).start()
+
+    @pl.loop(0, chunks + hops - 1)
+    def _(wave):
+        @pl.when(wave + AHEAD < chunks)
+        def _():
+            start_own(wave + AHEAD)
+
+        @pl.when(wave < chunks)
+        def _():
+            compute(me, wave)
+
+        @pl.when(jnp.logical_and(inner, wave == chunks + hops - 2))
+        def _():
+            @pl.loop(0, FIRST)
+            def _(i):
+                send_turn(i)
+
+        @pl.when(jnp.logical_and(wave > hops, wave < chunks + hops - 2))
+        def _():
+            attend(wave - hops - 1)
+
+        @pl.loop(1, hops + 1)
+        def _(hop):
+            c = wave - (hop - 1)
+            last = hop == hops
+
+            @pl.when(jnp.logical_and(c >= 0, c < chunks))
+            def _():
+                for way in range(2):
+                    @pl.when(jnp.logical_not(last))
+                    def _():
+                        ring_copy(way, hop, c, False).wait_recv()
+
+                    @pl.when(last)
+                    def _():
+                        ring_copy(way, hop, c, True).wait_recv()
+
+                    @pl.when(jnp.logical_or(hop < hops - 2, jnp.logical_and(hop == hops - 2, through(way))))
+                    def _():
+                        ring_copy(way, hop + 1, c, False).start()
+
+                    @pl.when(jnp.logical_and(hop == hops - 1, through(way)))
+                    def _():
+                        ring_copy(way, hop + 1, c, True).start()
+
+                    @pl.when(jnp.logical_and(jnp.logical_and(inner, out_way == way), hop == 1))
+                    def _():
+                        short_copy(1, c).start()
+
+                @pl.when(jnp.logical_and(inner, hop == SLOT_INNER))
+                def _():
+                    @pl.loop(c * EARLY_INNER // chunks, (c + 1) * EARLY_INNER // chunks)
+                    def _(k):
+                        wo_copy(1, k).start()
+
+                @pl.when(jnp.logical_and(corner, hop == SLOT_CORNER))
+                def _():
+                    wo_range(c * EARLY_CORNER // chunks, (c + 1) * EARLY_CORNER // chunks)
+
+                @pl.when(jnp.logical_and(c == chunks - 1, hop == hops - 1))
+                def _():
+                    attend(chunks - 3)
+
+                    @pl.when(corner)
+                    def _():
+                        wo_range(EARLY_CORNER, EARLY_CORNER + MORE)
+
+                @pl.loop(0, jnp.where(last, 1, 2))
+                def _(way):
+                    compute(ring_member(jnp.where(way == 0, position - hop, position + hop), n), c)
+
+        @pl.when(wave >= hops - 1)
+        def _():
+            project(wave - (hops - 1))
+
+    @pl.loop(START, turns + LEAD)
     def _(i):
         @pl.when(jnp.logical_or(i == LAST - 1, i == LAST))
         def _():
@@ -677,7 +704,7 @@
 
         @pl.when(jnp.logical_and(corner, i == LAST))
         def _():
-            wo_range(EARLY_CORNER, 2 * pieces)
+            wo_range(EARLY_CORNER + MORE, 2 * pieces)
 
         @pl.when(inner)
         def _():
@@ -687,20 +714,9 @@
                 def _(k):
                     wo_copy(1, k).start()
 
-            @pl.when(i < turns)
-            def _():
-                part, k = turn_of(i)
-
-                @pl.when(jnp.where(i < turns // 2, i < pieces // 2, part == 0))
-                def _():
-                    wo_own_copy(k).wait()
-                    for s in range(slots):
-                        @pl.when(slot != s)
-                        def _():
-                            wo_arrived(s, k).wait_recv()
-                contexts_arrived(1 - half, i)
-                leaving[i] = term(1 - half, part, k).astype(jnp.bfloat16)
-                mid_copy(i).start()
+            @pl.when(jnp.logical_and(i >= FIRST, i < turns))
+            def _():
+                send_turn(i)
 
             @pl.when(i >= LEAD)
             def _():

time: 216 us -> 215 us (level)
    pallas_call x1, Pallas kernels: 211 us -> 209 us  [local(): pl.pallas_call(functools.partial(kernel, n, chunks, pieces), name='layer'...]
where the time goes in v4:
time: 215 us; the launch traced here: 211 us
  Pallas kernels  209 us (97%)
  local copies, waits for them, and re-layouts  2.29 us (1%)
    pallas_call x1, Pallas kernels, local(): pl.pallas_call(functools.partial(kernel, n, chunks, pieces), name='layer'...  209 us

profile of v4, /device:TPU:4, one launch (start us, length us, event | category | flops | bytes accessed | tf_op | source)
XLA Modules:
  0.0 211.5 jit_solution(1796876429591875791)
XLA Ops:
  0.6 208.6 %layer.1 = (bf16[96,8192]{1,0:T(8,128)(2,1)S(1)}, bf16[96,8192]{1,0:T(8,128)(2,1)S(1)}) custom-call(bf16[768,1024]{1,0:T(8,128)(2,1)} %bitcast.14, bf16[8,1,1024]{2,1,0:T(2,128)(2,1)} %bitcast.15, bf16[256,8192]{1,0:T(8,128)(2,1)} %bitcast.10, bf16[128,8192]{1,0:T(8,128)(2,1)} %bitcast.12, bf16[128,8192]{1,0:T(8,128)(2,1)} %bitcast.13, ...), custom_call_target="tpu_custom_call" | custom-call | tf_op jit(solution)/shard_map/layer/pallas_call | solution.py:919
  209.2 1.1 copy.11
  210.4 1.1 copy.12

commit v5 on v4

--- a/solution.py
+++ b/solution.py
@@ -24,7 +24,7 @@
 SLOT_INNER = 2
 EARLY_CORNER = 7
 EARLY_INNER = 5
-MORE = 1
+MORE = 0
 HEAD = 3
 
 

time: 215 us -> 213 us (level)
  no operation moved by 1% of the time
where the time goes in v5:
time: 213 us; the launch traced here: 210 us
  Pallas kernels  207 us (97%)
  local copies, waits for them, and re-layouts  2.29 us (1%)
    pallas_call x1, Pallas kernels, local(): pl.pallas_call(functools.partial(kernel, n, chunks, pieces), name='layer'...  207 us

profile of v5, /device:TPU:4, one launch (start us, length us, event | category | flops | bytes accessed | tf_op | source)
XLA Modules:
  0.0 209.7 jit_solution(257101813637418225)
XLA Ops:
  0.6 206.8 %layer.1 = (bf16[96,8192]{1,0:T(8,128)(2,1)S(1)}, bf16[96,8192]{1,0:T(8,128)(2,1)S(1)}) custom-call(bf16[768,1024]{1,0:T(8,128)(2,1)} %bitcast.14, bf16[8,1,1024]{2,1,0:T(2,128)(2,1)} %bitcast.15, bf16[256,8192]{1,0:T(8,128)(2,1)} %bitcast.10, bf16[128,8192]{1,0:T(8,128)(2,1)} %bitcast.12, bf16[128,8192]{1,0:T(8,128)(2,1)} %bitcast.13, ...), custom_call_target="tpu_custom_call" | custom-call | tf_op jit(solution)/shard_map/layer/pallas_call | solution.py:919
  207.4 1.1 copy.11
  208.6 1.1 copy.12
